TPU v7x, 128 devices: a whole 4x4x4 slice. The times are simulated.
128 devices in a mesh: dp: 128 (over x, z, y, core).
Axes of the slice: x: 4, y: 4, z: 4, core: 2. Of those that a mesh axis runs over, the one named last changes fastest.
Arguments:
- gradients: bfloat16 [128, 256, 5120], P('dp'), may hold values from -6 to 6
- momentum: bfloat16 [256, 5120], replicated, may hold values from -6 to 6
- worker_error: bfloat16 [128, 256, 5120], P('dp'), may hold values from -1.796875 to 1.796875
- server_error: bfloat16 [256, 5120], P('dp'), may hold values from -1.796875 to 1.796875
- params: float32 [256, 5120], replicated, may hold values from -6 to 6
- variance: bfloat16 [256, 5120], replicated, may hold values from 0.099609375 to 4
Outputs:
- params_next: float32 [256, 5120], replicated
- momentum_next: bfloat16 [256, 5120], replicated
- worker_next: bfloat16 [128, 256, 5120], P('dp')
- server_next: bfloat16 [256, 5120], P('dp')
All inputs are finite; a program needn't handle non-finite values.
Results may differ from a plain program's by a relative error of at most 0.0082.
Values may be sent and summed in bfloat16 or wider, within the bound.
A program may use at most 128 MiB of HBM per device.

v0:
```python
import jax
import jax.numpy as jnp
from jax import lax
from jax.sharding import Mesh
from jax.sharding import PartitionSpec as P

DP = ("dp_0", "dp_1", "dp_2", "dp_3")


def from_everyone(x, axis):
    length = lax.axis_size(axis)
    return lax.all_to_all(jnp.broadcast_to(x[None], (length, *x.shape)), axis, 0, 0, tiled=True)


def joined_along(tiles, dim):
    lengths = list(tiles.shape[1:])
    lengths[dim] *= tiles.shape[0]
    return jnp.moveaxis(tiles, 0, dim).reshape(lengths)


def whole_of(x, axes, dim):
    far, near = axes
    leading = from_everyone(x, far)
    tiles = jnp.swapaxes(from_everyone(leading, near), 0, 1)
    return joined_along(tiles.reshape(-1, *x.shape), dim)


def to_scale(blocks):
    rounded = jnp.sqrt(jnp.mean(blocks * blocks, axis=1)).astype(jnp.bfloat16)
    rounded = lax.optimization_barrier(rounded)
    return rounded.astype(jnp.float32)


def local(gradients, momentum, worker_error, server_error, params, variance):
    devices = lax.axis_size(DP)
    row_count, features = momentum.shape
    row_owned = row_count // devices
    combined = (
        0.875 * momentum.astype(jnp.float32)
        + 0.125 * gradients[0].astype(jnp.float32)
        + worker_error[0].astype(jnp.float32)
    )
    blocks = combined.reshape(devices, row_owned * features)
    group_scale = to_scale(blocks)
    compressed = jnp.where(blocks >= 0, 1.0, -1.0).astype(jnp.float32) * group_scale[:, None]
    worker_next = (blocks - compressed).reshape(1, row_count, features).astype(jnp.bfloat16)
    outgoing = compressed.astype(jnp.bfloat16).reshape(devices, row_owned, features)
    received = lax.all_to_all(outgoing, DP, split_axis=0, concat_axis=0, tiled=True)
    summed = jnp.sum(received.astype(jnp.float32), axis=0)
    averaged = summed / devices
    served = (averaged + server_error.astype(jnp.float32)).reshape(1, row_owned * features)
    server_scale = to_scale(served)
    owner_comp = jnp.where(served >= 0, 1.0, -1.0).astype(jnp.float32) * server_scale[:, None]
    server_next = (served - owner_comp).reshape(row_owned, features).astype(jnp.bfloat16)
    owner_block = owner_comp.reshape(row_owned, features).astype(jnp.bfloat16)
    momentum_next = whole_of(owner_block, (("dp_0", "dp_1", "dp_2"), "dp_3"), 0)
    denom = jnp.sqrt(variance.astype(jnp.float32)) + 1e-08
    params_next = params - 0.5 * momentum_next.astype(jnp.float32) / denom
    return (params_next, momentum_next, worker_next, server_next)


def solution(mesh):
    split = Mesh(mesh.devices.reshape(4, 4, 4, 2), ("dp_0", "dp_1", "dp_2", "dp_3"))
    in_specs = (P(DP, None, None), P(), P(DP, None, None), P(DP, None), P(), P())
    out_specs = (P(), P(), P(DP, None, None), P(DP, None))
    return jax.shard_map(local, mesh=split, in_specs=in_specs, out_specs=out_specs, check_vma=False)
```

profile of v0, /device:TPU:1, one launch (start us, length us, event | category | flops | bytes accessed | tf_op | source)
XLA Modules:
  0.0 122.9 jit_solution(10338725262562757743)
XLA Ops:
  0.6 0.0 copy-start
  0.6 5.1 %multiply_reduce_fusion = f32[256]{0:T(256)S(1)} fusion(bf16[1,256,5120]{2,1,0:T(8,128)(2,1)} %param.8, bf16[1,256,5120]{2,1,0:T(8,128)(2,1)} %param.6, bf16[256,5120]{1,0:T(8,128)(2,1)} %param.7), kind=kLoop, calls=%fused_computation.6 | loop fusion | flops 11796224 | bytes 7865344 | tf_op jit(solution)/shard_map/reduce_sum | solution.py:29
  5.7 0.1 reduce_sum.35
  5.8 0.1 reduce_sum.36
  6.0 0.1 mul.81
  6.0 0.2 mul.82
  6.2 0.0 copy-done
  6.2 6.0 %fusion = (bf16[1,256,5120]{2,1,0:T(8,128)(2,1)}, f32[256,5120]{1,0:T(8,128)}) fusion(f32[256]{0:T(256)S(1)} %mul.82, bf16[1,256,5120]{2,1,0:T(8,128)(2,1)S(1)} %copy-done, bf16[1,256,5120]{2,1,0:T(8,128)(2,1)} %param.6, bf16[256,5120]{1,0:T(8,128)(2,1)} %param.7), kind=kLoop, calls=%fused_computation.8 | loop fusion | flops 15728640 | bytes 15729664 | tf_op jit(solution)/shard_map/convert_element_type | solution.py:46
  12.2 7.2 %select_n.19 = f32[128,2,5120]{2,1,0:T(2,128)} reshape(f32[256,5120]{1,0:T(8,128)} %get-tuple-element.5) | data formatting | bytes 10485760 | tf_op jit(solution)/shard_map/jit(_where)/select_n | solution.py:45
  19.4 4.7 %multiply_convert_fusion = bf16[128,2,5120]{2,1,0:T(2,128)(2,1)S(1)} fusion(f32[128,2,5120]{2,1,0:T(2,128)} %select_n.19, f32[128]{0:T(128)S(1)} %convert_element_type.59), kind=kLoop, calls=%fused_computation.5 | loop fusion | flops 2621440 | bytes 7864832 | tf_op jit(solution)/shard_map/convert_element_type | solution.py:47
  24.1 0.0 copy-start.1
  24.1 47.2 %all_to_all.15 = bf16[128,2,5120]{2,1,0:T(2,128)(2,1)S(1)} all-to-all(bf16[128,2,5120]{2,1,0:T(2,128)(2,1)S(1)} %multiply_convert_fusion), channel_id=1, replica_groups=mesh['dp_0'=4,'dp_1'=4,'dp_2'=4,'dp_3'=2] {'dp_0','dp_1','dp_2','dp_3'}, dimensions={0} | all-to-all | bytes 5242880 | tf_op jit(solution)/shard_map/all_to_all | solution.py:48
  71.3 2.1 %convert_reduce_fusion = f32[2,5120]{1,0:T(2,128)S(1)} fusion(bf16[128,2,5120]{2,1,0:T(2,128)(2,1)S(1)} %all_to_all.15), kind=kLoop, calls=%fused_computation.4 | loop fusion | flops 2611200 | bytes 2662400 | tf_op jit(solution)/shard_map/reduce_sum | solution.py:49
  73.4 0.0 copy-done.1
  73.4 0.6 multiply_reduce_fusion.1
  74.8 0.7 subtract_convert_fusion.1
  75.5 0.7 broadcast_in_dim.34
  76.1 23.4 %all_to_all.16 = bf16[64,2,5120]{2,1,0:T(2,128)(2,1)S(1)} all-to-all(bf16[64,2,5120]{2,1,0:T(2,128)(2,1)S(1)} %broadcast_in_dim.34), channel_id=1, replica_groups=mesh['dp_0'=4,'dp_1'=4,'dp_2'=4,'dp_3'=2] {'dp_0','dp_1','dp_2'}, dimensions={0} | all-to-all | bytes 2621440 | tf_op jit(solution)/shard_map/all_to_all | solution.py:12
  99.6 1.4 %broadcast_in_dim.35 = bf16[2,64,2,5120]{3,2,1,0:T(2,128)(2,1)S(1)} broadcast(bf16[64,2,5120]{2,1,0:T(2,128)(2,1)S(1)} %all_to_all.16), dimensions={1,2,3} | broadcast | bytes 3932160 | tf_op jit(solution)/shard_map/broadcast_in_dim | solution.py:12
  100.9 8.9 %all_to_all.17 = bf16[2,64,2,5120]{3,2,1,0:T(2,128)(2,1)S(1)} all-to-all(bf16[2,64,2,5120]{3,2,1,0:T(2,128)(2,1)S(1)} %broadcast_in_dim.35), channel_id=1, replica_groups=mesh['dp_0'=4,'dp_1'=4,'dp_2'=4,'dp_3'=2] {'dp_3'}, dimensions={0} | all-to-all | bytes 5242880 | tf_op jit(solution)/shard_map/all_to_all | solution.py:12
  109.9 1.8 %copy.10 = bf16[64,2,2,5120]{3,2,1,0:T(2,128)(2,1)S(1)} copy(bf16[64,2,2,5120]{3,2,0,1:T(2,128)(2,1)S(1)} %bitcast.25) | data formatting | bytes 5242880 | tf_op jit(solution)/shard_map/transpose | solution.py:24
  111.7 2.4 %reshape_reshape.3 = bf16[256,5120]{1,0:T(8,128)(2,1)} reshape(bf16[64,2,2,5120]{3,2,1,0:T(2,128)(2,1)S(1)} %copy.10) | data formatting | bytes 5242880 | tf_op jit(solution)/shard_map/reshape;reshape | solution.py:18
  114.1 8.8 %divide_subtract_fusion = f32[256,5120]{1,0:T(8,128)} fusion(f32[256,5120]{1,0:T(8,128)} %param.10, bf16[256,5120]{1,0:T(8,128)(2,1)} %param.11, bf16[256,5120]{1,0:T(8,128)(2,1)} %reshape_reshape.3), kind=kLoop, calls=%fused_computation.3 | loop fusion | flops 7864320 | bytes 15728640 | tf_op jit(solution)/shard_map/sub | solution.py:58
  (2 shorter events, 0.0 us)
Async XLA Ops:
  0.6 5.6 %copy-start = (bf16[1,256,5120]{2,1,0:T(8,128)(2,1)S(1)}, bf16[1,256,5120]{2,1,0:T(8,128)(2,1)}, u32[]{:S(2)}) copy-start(bf16[1,256,5120]{2,1,0:T(8,128)(2,1)} %param.8) | copy-start | bytes 7864324
  24.1 49.3 %copy-start.1 = (bf16[2,5120]{1,0:T(2,128)(2,1)S(1)}, bf16[2,5120]{1,0:T(2,128)(2,1)}, u32[]{:S(2)}) copy-start(bf16[2,5120]{1,0:T(2,128)(2,1)} %param.9) | copy-start | bytes 61444
where the time goes:
time: 123 us
  blocking collectives  79.6 us (65%)
  other arithmetic  28 us (23%)
  local copies, waits for them, and re-layouts  13.8 us (11%)
  between operations  1.41 us (1%)
    all_to_all x1, blocking collectives, local(): lax.all_to_all(outgoing, DP, split_axis=0, concat_axis=0, tiled=True)  47.2 us
    all_to_all x2, blocking collectives, from_everyone(): lax.all_to_all(jnp.broadcast_to(x[None], (length, *x.shape)), axis, 0, 0,...  32.4 us
    sub x1, other arithmetic, local(): params_next = params - 0.5 * momentum_next.astype(jnp.float32) / denom  8.76 us
    select_n x1, local copies, waits for them, and re-layouts, local(): jnp.where(blocks >= 0, 1.0, -1.0).astype(jnp.float32) * group_scale[:, None]  7.2 us
    convert_element_type x1, other arithmetic, local(): (blocks - compressed).reshape(1, row_count, features).astype(jnp.bfloat16)  5.99 us
    reduce_sum x3, other arithmetic, to_scale(): rounded = jnp.sqrt(jnp.mean(blocks * blocks, axis=1)).astype(jnp.bfloat16)  5.8 us
    convert_element_type x1, other arithmetic, local(): compressed.astype(jnp.bfloat16).reshape(devices, row_owned, features)  4.69 us

commit v1 on v0

v1 whole, which is shorter than its diff:
```python
import jax
import jax.numpy as jnp
from jax import lax
from jax.experimental import pallas as pl
from jax.experimental.pallas import tpu as pltpu
from jax.sharding import Mesh
from jax.sharding import PartitionSpec as P

MESH = pl.DeviceIdType.MESH
F32, BF16 = jnp.float32, jnp.bfloat16
DP = ("dp_0", "dp_1", "dp_2", "dp_3")
ORDERS = ((0, 1, 2), (1, 2, 0), (2, 0, 1))
ROWS, COLS, N_DEV = 256, 5120, 128
LANES = 128
W = 7 * LANES
WIDTHS = (W, W, W, W, W, COLS - 5 * W)
N_BLOCK = (ROWS // N_DEV) * COLS
N_SEND = 132


def lane_tile(start):
    return pl.ds(pl.multiple_of(start, LANES), LANES)


def swap_granules(tiles):
    low = lax.broadcasted_iota(jnp.int32, (8, LANES), 0) < 4
    swapped = []
    for i in range(4):
        pairs = []
        for first, second in ((tiles[0], tiles[1]), (tiles[2], tiles[3])):
            a, b = first[i // 2], second[i // 2]
            if i % 2 == 0:
                pairs.append(jnp.where(low, a, pltpu.roll(b, 4, 0)))
            else:
                pairs.append(jnp.where(low, pltpu.roll(a, 4, 0), b))
        swapped.append(pairs)
    return swapped


def compress_kernel(g_hbm, m_hbm, e_hbm, w_hbm, o_ref, g, m, e, comb, scale, w, in_sem, out_sem):
    chunk = 32
    loads = []
    for i in range(ROWS // chunk):
        rows = pl.ds(i * chunk, chunk)
        group = []
        for n, (src, dst) in enumerate(((g_hbm, g), (m_hbm, m), (e_hbm, e))):
            copy = pltpu.make_async_copy(src.at[rows], dst.at[rows], in_sem.at[n, i])
            copy.start()
            group.append(copy)
        loads.append(group)

    even = lax.broadcasted_iota(jnp.int32, (8, LANES), 0) % 2 == 0
    for i in range(ROWS // chunk):
        for copy in loads[i]:
            copy.wait()
        rows = pl.ds(i * chunk, chunk)

        def square(t, acc):
            cols = lane_tile(t * LANES)
            value = (
                0.875 * m[rows, cols].astype(F32)
                + 0.125 * g[rows, cols].astype(F32)
                + e[rows, cols].astype(F32)
            )
            comb[rows, cols] = value
            return acc + value * value

        acc = lax.fori_loop(0, COLS // LANES, square, jnp.zeros((chunk, LANES), F32), unroll=4)
        for s in range(chunk // 8):
            row = jnp.sum(acc[8 * s : 8 * s + 8], axis=1, keepdims=True)
            row = jnp.broadcast_to(row, (8, LANES))
            both = row + jnp.where(even, pltpu.roll(row, 7, 0), pltpu.roll(row, 1, 0))
            rounded = jnp.sqrt(both * (1.0 / N_BLOCK)).astype(BF16)
            scale[pl.ds(i * chunk + 8 * s, 8)] = rounded.astype(F32)

    stores = []
    for piece in range(6):
        k, h = divmod(piece, 2)

        def column(j, carry, piece=piece, k=k, h=h):
            src, dst = lane_tile(piece * W + j * LANES), lane_tile(j * LANES)
            for outer in range(4):
                tiles = []
                for inner in range(4):
                    x, z = (inner, outer) if k == 1 else (outer, inner)
                    top = 16 * (4 * x + z)
                    parts, rests = [], []
                    for s in range(2):
                        rows = pl.ds(top + 8 * s, 8)
                        value, size = comb[rows, src], scale[rows]
                        part = jnp.where(value >= 0, size, -size)
                        parts.append(part)
                        rests.append(value - part)
                    w[pl.ds(top, 16), src] = jnp.concatenate(rests, 0).astype(BF16)
                    tiles.append(parts)
                if k != 0:
                    tiles = swap_granules(tiles)
                for i in range(4):
                    far, near = (i, outer) if k == 2 else (outer, i)
                    half, row = 2 * far + near // 2, (near % 2) * 16
                    o_ref[k, h, half, pl.ds(row, 16), dst] = jnp.concatenate(tiles[i], 0).astype(BF16)
            return carry

        lax.fori_loop(0, WIDTHS[piece] // LANES, column, 0)
        if WIDTHS[piece] < W:
            rest = W - WIDTHS[piece]
            for half in range(8):
                o_ref[k, h, half, :, pl.ds(WIDTHS[piece], rest)] = jnp.zeros((32, rest), BF16)
        cols = pl.ds(piece * W, WIDTHS[piece])
        copy = pltpu.make_async_copy(w.at[:, cols], w_hbm.at[:, cols], out_sem.at[piece])
        copy.start()
        stores.append(copy)
    for copy in stores:
        copy.wait()


def exchange_kernel(
    o, se, m, sn,
    ra, rd, ro, rb1, rb2, sb2, s1, r2, st, s2, r3, sv, mb, rq,
    send_sem, ra_sem, rd_sem, rb1_sem, rb2_sem, r2_sem, r3_sem, rq_sem, q2_sem, q3_sem, d_sem,
):
    pos = [lax.axis_index(DP[a]) for a in range(3)]
    c = lax.axis_index(DP[3])
    other = 1 - c

    def step(v, d):
        return lax.rem(v + d, 4)

    def device(axis, delta, core):
        at = list(pos)
        if delta:
            at[axis] = step(pos[axis], delta)
        return (*at, core)

    sent = []

    def push(src, dst, sem, to):
        copy = pltpu.make_async_remote_copy(
            src_ref=src, dst_ref=dst, send_sem=send_sem.at[len(sent)], recv_sem=sem,
            device_id=to, device_id_type=MESH,
        )
        copy.start()
        sent.append(copy)

    def arrived(dst, sem):
        pltpu.make_async_remote_copy(
            src_ref=dst, dst_ref=dst, send_sem=send_sem.at[0], recv_sem=sem,
            device_id=device(0, 0, other), device_id_type=MESH,
        ).wait_recv()

    barrier = pltpu.get_barrier_semaphore()
    peers = [device(0, 0, other)]
    for axis in range(3):
        for delta in (1, 3, 2):
            for core in range(2):
                peers.append(device(axis, delta, core))
    for peer in peers:
        pl.semaphore_signal(barrier, inc=1, device_id=peer, device_id_type=MESH)
    pl.semaphore_wait(barrier, len(peers))

    partner = device(0, 0, other)
    ring = [tuple(step(pos[order[0]], d) for d in range(4)) for order in ORDERS]

    for k, order in enumerate(ORDERS):
        p2 = ring[k][2]
        for h in range(2):
            push(o.at[k, h, 2 * p2], ra.at[k, 0, c], ra_sem.at[k, 0, c], device(order[0], 1, h))
            push(o.at[k, h, 2 * p2 + 1], ra.at[k, 1, c], ra_sem.at[k, 1, c], device(order[0], 3, h))
    for k, order in enumerate(ORDERS):
        p, p1, _, p3 = ring[k]
        push(o.at[k, other, 2 * p1], rd.at[k, 0], rd_sem.at[k, 0], partner)
        push(o.at[k, other, 2 * p3 + 1], rd.at[k, 1], rd_sem.at[k, 1], partner)
    for k, order in enumerate(ORDERS):
        p, p1, _, p3 = ring[k]
        for h in range(2):
            push(o.at[k, h, 2 * p1 + 1], rb1.at[k, 0, c], rb1_sem.at[k, 0, c], device(order[0], 1, h))
            push(o.at[k, h, 2 * p3], rb1.at[k, 1, c], rb1_sem.at[k, 1, c], device(order[0], 3, h))
    for k in range(3):
        push(o.at[k, other, pl.ds(2 * ring[k][0], 2)], ro.at[k], rd_sem.at[k, 2], partner)
    for k, order in enumerate(ORDERS):
        p, p1, _, p3 = ring[k]
        for d in range(2):
            arrived(rd.at[k, d], rd_sem.at[k, d])
            for core in range(2):
                arrived(ra.at[k, d, core], ra_sem.at[k, d, core])
            for half in range(2):
                rows = pl.ds(16 * half, 16)
                sb2[k, d, rows] = (
                    (o[k, c, 2 * p1 if d == 0 else 2 * p3 + 1, rows].astype(F32) + rd[k, d, rows].astype(F32))
                    + (ra[k, d, 0, rows].astype(F32) + ra[k, d, 1, rows].astype(F32))
                )
            push(sb2.at[k, d], rb2.at[k, d], rb2_sem.at[k, d], device(order[0], 1 if d == 0 else 3, c))

    for k, order in enumerate(ORDERS):
        p, q = ring[k][0], pos[order[1]]
        arrived(ro.at[k], rd_sem.at[k, 2])
        for d in range(2):
            for core in range(2):
                arrived(rb1.at[k, d, core], rb1_sem.at[k, d, core])
        for d in range(2):
            arrived(rb2.at[k, d], rb2_sem.at[k, d])
            for half in range(2):
                rows = pl.ds(16 * half, 16)
                s1[k, 2 * d + half] = (
                    (o[k, c, 2 * p + d, rows].astype(F32) + ro[k, d, rows].astype(F32))
                    + (rb1[k, 1 - d, 0, rows].astype(F32) + rb1[k, 1 - d, 1, rows].astype(F32))
                    + rb2[k, d, rows]
                )
        for delta in (2, 1, 3):
            push(
                s1.at[k, step(q, delta)], r2.at[k, delta - 1], r2_sem.at[k, delta - 1], device(order[1], delta, c)
            )

    for k, order in enumerate(ORDERS):
        q, r = pos[order[1]], pos[order[2]]
        for delta in range(1, 4):
            arrived(r2.at[k, delta - 1], r2_sem.at[k, delta - 1])
        st[k] = (s1[k, q] + r2[k, 0]) + (r2[k, 1] + r2[k, 2])
        for i in range(8):
            s2[k, i] = st[k, pl.ds(2 * i, 2), :]
        for delta in (2, 1, 3):
            for core in range(2):
                push(
                    s2.at[k, 2 * step(r, delta) + core], r3.at[k, delta, c], r3_sem.at[k, delta, c],
                    device(order[2], delta, core),
                )
        push(s2.at[k, 2 * r + other], r3.at[k, 0, c], r3_sem.at[k, 0, c], partner)
        r3[k, 0, c] = s2[k, 2 * r + c]

    squares = jnp.zeros((2, LANES), F32)
    for piece in range(6):
        k, h = divmod(piece, 2)
        if h == 0:
            arrived(r3.at[k, 0, other], r3_sem.at[k, 0, other])
            for delta in range(1, 4):
                for core in range(2):
                    arrived(r3.at[k, delta, core], r3_sem.at[k, delta, core])
        width = WIDTHS[piece]
        cols = pl.ds(0, width)
        total = (r3[k, 0, h, :, cols] + r3[k, 1, h, :, cols]) + (r3[k, 2, h, :, cols] + r3[k, 3, h, :, cols])
        served = total * (1.0 / N_DEV) + se[:, pl.ds(piece * W, width)].astype(F32)
        sv[piece, :, cols] = served
        for t in range(width // LANES):
            part = served[:, t * LANES : (t + 1) * LANES]
            squares = squares + part * part
    total = jnp.sum(jnp.sum(squares, axis=1, keepdims=True), axis=0, keepdims=True)
    size = jnp.sqrt(total * (1.0 / N_BLOCK)).astype(BF16).astype(F32)
    for piece in range(6):
        k, h = divmod(piece, 2)
        width = WIDTHS[piece]
        cols = pl.ds(0, width)
        served = sv[piece, :, cols]
        level = jnp.broadcast_to(size, (2, width))
        comp = jnp.where(served >= 0, level, -level)
        sn[:, pl.ds(piece * W, width)] = (served - comp).astype(BF16)
        mb[k, h, :, cols] = comp.astype(BF16)
        if width < W:
            mb[k, h, :, pl.ds(width, W - width)] = jnp.zeros((2, W - width), BF16)

    for k, order in enumerate(ORDERS):
        r = pos[order[2]]
        mine = 2 * r + c
        for delta in (2, 1, 3):
            for h in range(2):
                push(mb.at[k, h], rq.at[k, mine], rq_sem.at[k, mine], device(order[2], delta, h))
        push(mb.at[k, other], rq.at[k, mine], rq_sem.at[k, mine], partner)
        rq[k, mine] = mb[k, c]
    for k, order in enumerate(ORDERS):
        p, q, r = (pos[a] for a in order)
        arrived(rq.at[k, 2 * r + other], rq_sem.at[k, 2 * r + other])
        for delta in range(1, 4):
            for core in range(2):
                at = 2 * step(r, delta) + core
                arrived(rq.at[k, at], rq_sem.at[k, at])
        for i in range(8):
            st[k, pl.ds(2 * i, 2), :] = rq[k, i].astype(F32)
        m[k, c, p, q] = st[k].astype(BF16)
        for delta in (2, 1, 3):
            push(m.at[k, c, p, q], m.at[k, c, p, q], q2_sem.at[k, q], device(order[1], delta, c))
    for k, order in enumerate(ORDERS):
        p, q = pos[order[0]], pos[order[1]]
        for delta in range(1, 4):
            at = step(q, delta)
            arrived(m.at[k, c, p, at], q2_sem.at[k, at])
        for d in range(2):
            for half in (d, 1 - d):
                view = m.at[k, c, p, pl.ds(2 * half, 2)]
                push(view, view, q3_sem.at[k, d, half], device(order[0], 1 if d == 0 else 3, c))
        push(m.at[k, c, p], m.at[k, c, p], d_sem.at[k, 0], partner)
    for k, order in enumerate(ORDERS):
        _, p1, _, p3 = ring[k]
        for d in range(2):
            view = m.at[k, c, p3 if d == 0 else p1, pl.ds(2 * d, 2)]
            arrived(view, q3_sem.at[k, d, d])
            push(view, view, q3_sem.at[k, d, 2], device(order[0], 1 if d == 0 else 3, c))
    for k in range(3):
        _, p1, _, p3 = ring[k]
        for d in range(2):
            at = p3 if d == 0 else p1
            arrived(m.at[k, c, at, pl.ds(2 * (1 - d), 2)], q3_sem.at[k, d, 1 - d])
            push(m.at[k, c, at], m.at[k, c, at], d_sem.at[k, 1 + d], partner)
    for k in range(3):
        p2 = ring[k][2]
        for d in range(2):
            view = m.at[k, c, p2, pl.ds(2 * d, 2)]
            arrived(view, q3_sem.at[k, d, 2])
            push(view, view, d_sem.at[k, 3 + d], partner)
    for k in range(3):
        p, p1, p2, p3 = ring[k]
        for n, at in enumerate((p, p3, p1)):
            arrived(m.at[k, other, at], d_sem.at[k, n])
        for d in range(2):
            arrived(m.at[k, other, p2, pl.ds(2 * d, 2)], d_sem.at[k, 3 + d])
    for copy in sent:
        copy.wait_send()


def update_kernel(m, params, variance, params_next, momentum_next):
    piece = pl.program_id(0)

    for k in range(3):

        @pl.when(piece // 2 == k)
        def _(k=k):
            def column(j, carry):
                cols = lane_tile(j * LANES)
                for outer in range(4):
                    tiles = []
                    for i in range(4):
                        far, near = (i, outer) if k == 2 else (outer, i)
                        tile = m[0, 0, far, near, :, cols].astype(F32)
                        tiles.append([tile[:8], tile[8:]])
                    if k != 0:
                        tiles = swap_granules(tiles)
                    for inner in range(4):
                        x, z = (inner, outer) if k == 1 else (outer, inner)
                        rows = pl.ds(16 * (4 * x + z), 16)
                        value = jnp.concatenate(tiles[inner], 0)
                        momentum_next[rows, cols] = value.astype(BF16)
                        denom = jnp.sqrt(variance[rows, cols].astype(F32)) + 1e-08
                        params_next[rows, cols] = params[rows, cols] - 0.5 * value / denom
                return carry

            lax.fori_loop(0, W // LANES, column, 0)


def local(gradients, momentum, worker_error, server_error, params, variance):
    hbm = pl.BlockSpec(memory_space=pl.ANY)
    vmem = pl.BlockSpec(memory_space=pltpu.VMEM)
    worker_next, outgoing = pl.pallas_call(
        compress_kernel,
        out_shape=(
            jax.ShapeDtypeStruct((ROWS, COLS), BF16),
            jax.ShapeDtypeStruct((3, 2, 8, 32, W), BF16),
        ),
        in_specs=[hbm] * 3,
        out_specs=(hbm, vmem),
        scratch_shapes=[
            pltpu.VMEM((ROWS, COLS), BF16),
            pltpu.VMEM((ROWS, COLS), BF16),
            pltpu.VMEM((ROWS, COLS), BF16),
            pltpu.VMEM((ROWS, COLS), F32),
            pltpu.VMEM((ROWS, LANES), F32),
            pltpu.VMEM((ROWS, COLS), BF16),
            pltpu.SemaphoreType.DMA((3, 8)),
            pltpu.SemaphoreType.DMA((6,)),
        ],
        compiler_params=pltpu.CompilerParams(vmem_limit_bytes=26 * 2**20),
        name="compress",
    )(gradients.reshape(ROWS, COLS), momentum, worker_error.reshape(ROWS, COLS))

    dma = pltpu.SemaphoreType.DMA
    gathered, server_next = pl.pallas_call(
        exchange_kernel,
        out_shape=(
            jax.ShapeDtypeStruct((3, 2, 4, 4, 16, W), BF16),
            jax.ShapeDtypeStruct((2, COLS), BF16),
        ),
        in_specs=[vmem, vmem],
        out_specs=(vmem, vmem),
        scratch_shapes=[
            pltpu.VMEM((3, 2, 2, 32, W), BF16),
            pltpu.VMEM((3, 2, 32, W), BF16),
            pltpu.VMEM((3, 2, 32, W), BF16),
            pltpu.VMEM((3, 2, 2, 32, W), BF16),
            pltpu.VMEM((3, 2, 32, W), F32),
            pltpu.VMEM((3, 2, 32, W), F32),
            pltpu.VMEM((3, 4, 16, W), F32),
            pltpu.VMEM((3, 3, 16, W), F32),
            pltpu.VMEM((3, 16, W), F32),
            pltpu.VMEM((3, 8, 2, W), F32),
            pltpu.VMEM((3, 4, 2, 2, W), F32),
            pltpu.VMEM((6, 2, W), F32),
            pltpu.VMEM((3, 2, 2, W), BF16),
            pltpu.VMEM((3, 8, 2, W), BF16),
            dma((N_SEND,)),
            dma((3, 2, 2)),
            dma((3, 3)),
            dma((3, 2, 2)),
            dma((3, 2)),
            dma((3, 3)),
            dma((3, 4, 2)),
            dma((3, 8)),
            dma((3, 4)),
            dma((3, 2, 3)),
            dma((3, 5)),
        ],
        compiler_params=pltpu.CompilerParams(
            collective_id=0, has_side_effects=True, vmem_limit_bytes=20 * 2**20
        ),
        name="exchange",
    )(outgoing, server_error)

    params_next, momentum_next = pl.pallas_call(
        update_kernel,
        grid=(6,),
        out_shape=(
            jax.ShapeDtypeStruct((ROWS, COLS), F32),
            jax.ShapeDtypeStruct((ROWS, COLS), BF16),
        ),
        in_specs=[
            pl.BlockSpec((1, 1, 4, 4, 16, W), lambda i: (i // 2, i % 2, 0, 0, 0, 0)),
            pl.BlockSpec((ROWS, W), lambda i: (0, i)),
            pl.BlockSpec((ROWS, W), lambda i: (0, i)),
        ],
        out_specs=(
            pl.BlockSpec((ROWS, W), lambda i: (0, i)),
            pl.BlockSpec((ROWS, W), lambda i: (0, i)),
        ),
        compiler_params=pltpu.CompilerParams(vmem_limit_bytes=16 * 2**20),
        name="update",
    )(gathered, params, variance)
    return (params_next, momentum_next, worker_next.reshape(1, ROWS, COLS), server_next)


def solution(mesh):
    split = Mesh(mesh.devices.reshape(4, 4, 4, 2), DP)
    in_specs = (P(DP, None, None), P(), P(DP, None, None), P(DP, None), P(), P())
    out_specs = (P(), P(), P(DP, None, None), P(DP, None))
    return jax.shard_map(local, mesh=split, in_specs=in_specs, out_specs=out_specs, check_vma=False)
```

time: 123 us -> 67 us (0.54)
  blocking collectives: 79.6 us -> 0 us
  Pallas kernels: 0 us -> 60 us
  other arithmetic: 28 us -> 0.01 us
  local copies, waits for them, and re-layouts: 13.8 us -> 6.13 us
    all_to_all x3 -> x0, blocking collectives: 79.6 us -> none  [the longest x1 47.2 us: local(): lax.all_to_all(outgoing, DP, split_axis=0, concat_axis=0, tiled=True)]
    pallas_call x0 -> x3, Pallas kernels: none -> 60 us  [the longest x1 45.4 us: local(): pl.pallas_call(exchange_kernel, out_shape=(jax.ShapeDtypeStruct((3, 2, 4,...]
    convert_element_type x5 -> x0, other arithmetic: 11.4 us -> none  [the longest x1 5.99 us: local(): (blocks - compressed).reshape(1, row_count, features).astype(jnp.bfloat16)]
    sub x1 -> x0, other arithmetic: 8.76 us -> none  [local(): params_next = params - 0.5 * momentum_next.astype(jnp.float32) / denom]
    reduce_sum x4 -> x0, other arithmetic: 7.9 us -> none  [the longest x3 5.8 us: to_scale(): rounded = jnp.sqrt(jnp.mean(blocks * blocks, axis=1)).astype(jnp.bfloat16)]
    select_n x1 -> x0, local copies, waits for them, and re-layouts: 7.2 us -> none  [local(): jnp.where(blocks >= 0, 1.0, -1.0).astype(jnp.float32) * group_scale[:, None]]
    unnamed x4 -> x15, local copies, waits for them, and re-layouts: 0.01 us -> 6.13 us
    another operation x1 -> x0, local copies, waits for them, and re-layouts: 2.44 us -> none  [joined_along(): return jnp.moveaxis(tiles, 0, dim).reshape(lengths)]
where the time goes in v1:
time: 67 us; the launch traced here: 66.8 us
  Pallas kernels  60 us (90%)
  local copies, waits for them, and re-layouts  6.13 us (9%)
  between operations  0.71 us (1%)
    pallas_call x1, Pallas kernels, local(): pl.pallas_call(exchange_kernel, out_shape=(jax.ShapeDtypeStruct((3, 2, 4,...  45.4 us
    pallas_call x1, Pallas kernels, local(): pl.pallas_call(compress_kernel, out_shape=(jax.ShapeDtypeStruct((ROWS, CO...  8.37 us
    pallas_call x1, Pallas kernels, local(): pl.pallas_call(update_kernel, grid=(6,), out_shape=(jax.ShapeDtypeStruct(...  6.21 us
    unnamed x15, local copies, waits for them, and re-layouts  6.13 us

profile of v1, /device:TPU:1, one launch (start us, length us, event | category | flops | bytes accessed | tf_op | source)
XLA Modules:
  0.0 66.8 jit_solution(13517226386965292012)
XLA Ops:
  0.6 0.0 slice-start
  0.6 0.0 copy-start
  0.7 1.9 %copy-done = bf16[1,256,5120]{2,1,0:T(8,128)(2,1)S(1)} copy-done((bf16[1,256,5120]{2,1,0:T(8,128)(2,1)S(1)}, bf16[1,256,5120]{2,1,0:T(8,128)(2,1)}, u32[]{:S(2)}) %copy-start) | copy-done | bytes 2621464
  2.5 0.0 copy-start.1
  2.5 1.9 %copy-done.1 = bf16[256,5120]{1,0:T(8,128)(2,1)S(1)} copy-done((bf16[256,5120]{1,0:T(8,128)(2,1)S(1)}, bf16[256,5120]{1,0:T(8,128)(2,1)}, u32[]{:S(2)}) %copy-start.1) | copy-done | bytes 2621464
  4.4 0.0 copy-start.2
  4.4 1.7 %copy-done.2 = bf16[1,256,5120]{2,1,0:T(8,128)(2,1)S(1)} copy-done((bf16[1,256,5120]{2,1,0:T(8,128)(2,1)S(1)}, bf16[1,256,5120]{2,1,0:T(8,128)(2,1)}, u32[]{:S(2)}) %copy-start.2) | copy-done | bytes 2621464
  6.2 0.0 copy-start.4
  6.2 0.0 slice-start.1
  6.2 8.4 %compress.1 = (bf16[256,5120]{1,0:T(8,128)(2,1)}, bf16[3,2,8,32,896]{4,3,2,1,0:T(8,128)(2,1)S(1)}) custom-call(bf16[256,5120]{1,0:T(8,128)(2,1)S(1)} %bitcast.5, bf16[256,5120]{1,0:T(8,128)(2,1)S(1)} %copy-done.1, bf16[256,5120]{1,0:T(8,128)(2,1)S(1)} %bitcast.6), custom_call_target="tpu_custom_call" | custom-call | tf_op jit(solution)/shard_map/compress/pallas_call | solution.py:350
  14.5 0.0 copy-start.3
  14.6 0.0 copy-done.4
  14.6 45.4 %exchange.1 = (bf16[3,2,4,4,16,896]{5,4,3,2,1,0:T(8,128)(2,1)S(1)}, bf16[2,5120]{1,0:T(2,128)(2,1)S(1)}) custom-call(bf16[3,2,8,32,896]{4,3,2,1,0:T(8,128)(2,1)S(1)} %get-tuple-element.10.o, bf16[2,5120]{1,0:T(2,128)(2,1)S(1)} %copy-done.4), custom_call_target="tpu_custom_call" | custom-call | tf_op jit(solution)/shard_map/exchange/pallas_call | solution.py:373
  60.0 0.0 slice-done
  60.0 0.0 slice-done.1
  60.0 0.0 copy-done.3
  60.0 6.2 %update.1 = (f32[256,5120]{1,0:T(8,128)}, bf16[256,5120]{1,0:T(8,128)(2,1)}) custom-call(bf16[3,2,4,4,16,896]{5,4,3,2,1,0:T(8,128)(2,1)S(1)} %get-tuple-element.11.m, f32[256,5120]{1,0:T(8,128)S(1)} %bitcast.4, bf16[256,5120]{1,0:T(8,128)(2,1)S(1)} %copy-done.3), custom_call_target="tpu_custom_call" | custom-call | tf_op jit(solution)/shard_map/update/pallas_call | solution.py:414
  66.2 0.6 copy.11
  (1 shorter events, 0.0 us)
Async XLA Ops:
  0.6 59.3 %slice-start = ((s8[5242880]{0:T(1024)(128)(4,1)}), s8[4194304]{0:T(1024)(128)(4,1)S(1)}, s32[]{:S(2)}) async-start(s8[5242880]{0:T(1024)(128)(4,1)} %bitcast.3), calls=%async_computation | async-start | bytes 8388608
  0.6 1.9 %copy-start = (bf16[1,256,5120]{2,1,0:T(8,128)(2,1)S(1)}, bf16[1,256,5120]{2,1,0:T(8,128)(2,1)}, u32[]{:S(2)}) copy-start(bf16[1,256,5120]{2,1,0:T(8,128)(2,1)} %param.6) | copy-start | bytes 7864324
  2.5 1.9 %copy-start.1 = (bf16[256,5120]{1,0:T(8,128)(2,1)S(1)}, bf16[256,5120]{1,0:T(8,128)(2,1)}, u32[]{:S(2)}) copy-start(bf16[256,5120]{1,0:T(8,128)(2,1)} %m_hbm.1) | copy-start | bytes 7864324
  4.4 1.7 %copy-start.2 = (bf16[1,256,5120]{2,1,0:T(8,128)(2,1)S(1)}, bf16[1,256,5120]{2,1,0:T(8,128)(2,1)}, u32[]{:S(2)}) copy-start(bf16[1,256,5120]{2,1,0:T(8,128)(2,1)} %param.8) | copy-start | bytes 7864324
  6.2 8.4 %copy-start.4 = (bf16[2,5120]{1,0:T(2,128)(2,1)S(1)}, bf16[2,5120]{1,0:T(2,128)(2,1)}, u32[]{:S(2)}) copy-start(bf16[2,5120]{1,0:T(2,128)(2,1)} %se.1) | copy-start | bytes 61444
  6.2 53.8 %slice-start.1 = ((s8[5242880]{0:T(1024)(128)(4,1)}), s8[1048576]{0:T(1024)(128)(4,1)S(1)}, s32[]{:S(2)}) async-start(s8[5242880]{0:T(1024)(128)(4,1)} %bitcast.3), calls=%async_computation.1 | async-start | bytes 2097152
  14.5 45.4 %copy-start.3 = (bf16[256,5120]{1,0:T(8,128)(2,1)S(1)}, bf16[256,5120]{1,0:T(8,128)(2,1)}, u32[]{:S(2)}) copy-start(bf16[256,5120]{1,0:T(8,128)(2,1)} %variance.1) | copy-start | bytes 7864324

commit v2 on v1

--- a/solution.py
+++ b/solution.py
@@ -16,6 +16,7 @@
 WIDTHS = (W, W, W, W, W, COLS - 5 * W)
 N_BLOCK = (ROWS // N_DEV) * COLS
 N_SEND = 132
+VMEM_STEP, VMEM_UPDATE = 26 * 2**20, 9 * 2**20
 
 
 def lane_tile(start):
@@ -37,86 +38,10 @@
     return swapped
 
 
-def compress_kernel(g_hbm, m_hbm, e_hbm, w_hbm, o_ref, g, m, e, comb, scale, w, in_sem, out_sem):
-    chunk = 32
-    loads = []
-    for i in range(ROWS // chunk):
-        rows = pl.ds(i * chunk, chunk)
-        group = []
-        for n, (src, dst) in enumerate(((g_hbm, g), (m_hbm, m), (e_hbm, e))):
-            copy = pltpu.make_async_copy(src.at[rows], dst.at[rows], in_sem.at[n, i])
-            copy.start()
-            group.append(copy)
-        loads.append(group)
-
-    even = lax.broadcasted_iota(jnp.int32, (8, LANES), 0) % 2 == 0
-    for i in range(ROWS // chunk):
-        for copy in loads[i]:
-            copy.wait()
-        rows = pl.ds(i * chunk, chunk)
-
-        def square(t, acc):
-            cols = lane_tile(t * LANES)
-            value = (
-                0.875 * m[rows, cols].astype(F32)
-                + 0.125 * g[rows, cols].astype(F32)
-                + e[rows, cols].astype(F32)
-            )
-            comb[rows, cols] = value
-            return acc + value * value
-
-        acc = lax.fori_loop(0, COLS // LANES, square, jnp.zeros((chunk, LANES), F32), unroll=4)
-        for s in range(chunk // 8):
-            row = jnp.sum(acc[8 * s : 8 * s + 8], axis=1, keepdims=True)
-            row = jnp.broadcast_to(row, (8, LANES))
-            both = row + jnp.where(even, pltpu.roll(row, 7, 0), pltpu.roll(row, 1, 0))
-            rounded = jnp.sqrt(both * (1.0 / N_BLOCK)).astype(BF16)
-            scale[pl.ds(i * chunk + 8 * s, 8)] = rounded.astype(F32)
-
-    stores = []
-    for piece in range(6):
-        k, h = divmod(piece, 2)
-
-        def column(j, carry, piece=piece, k=k, h=h):
-            src, dst = lane_tile(piece * W + j * LANES), lane_tile(j * LANES)
-            for outer in range(4):
-                tiles = []
-                for inner in range(4):
-                    x, z = (inner, outer) if k == 1 else (outer, inner)
-                    top = 16 * (4 * x + z)
-                    parts, rests = [], []
-                    for s in range(2):
-                        rows = pl.ds(top + 8 * s, 8)
-                        value, size = comb[rows, src], scale[rows]
-                        part = jnp.where(value >= 0, size, -size)
-                        parts.append(part)
-                        rests.append(value - part)
-                    w[pl.ds(top, 16), src] = jnp.concatenate(rests, 0).astype(BF16)
-                    tiles.append(parts)
-                if k != 0:
-                    tiles = swap_granules(tiles)
-                for i in range(4):
-                    far, near = (i, outer) if k == 2 else (outer, i)
-                    half, row = 2 * far + near // 2, (near % 2) * 16
-                    o_ref[k, h, half, pl.ds(row, 16), dst] = jnp.concatenate(tiles[i], 0).astype(BF16)
-            return carry
-
-        lax.fori_loop(0, WIDTHS[piece] // LANES, column, 0)
-        if WIDTHS[piece] < W:
-            rest = W - WIDTHS[piece]
-            for half in range(8):
-                o_ref[k, h, half, :, pl.ds(WIDTHS[piece], rest)] = jnp.zeros((32, rest), BF16)
-        cols = pl.ds(piece * W, WIDTHS[piece])
-        copy = pltpu.make_async_copy(w.at[:, cols], w_hbm.at[:, cols], out_sem.at[piece])
-        copy.start()
-        stores.append(copy)
-    for copy in stores:
-        copy.wait()
-
-
-def exchange_kernel(
-    o, se, m, sn,
-    ra, rd, ro, rb1, rb2, sb2, s1, r2, st, s2, r3, sv, mb, rq,
+def step_kernel(
+    g_hbm, m_hbm, e_hbm, se_hbm, p_hbm, v_hbm, m, sn, wn, rate, pv,
+    gv, mv, ev, vv, se, comb, scale, o, ra, rd, ro, rb1, rb2, sb2, s1, r2, st, s2, r3, sv, mb, rq,
+    in_sem, aux_sem,
     send_sem, ra_sem, rd_sem, rb1_sem, rb2_sem, r2_sem, r3_sem, rq_sem, q2_sem, q3_sem, d_sem,
 ):
     pos = [lax.axis_index(DP[a]) for a in range(3)]
@@ -156,14 +81,82 @@
                 peers.append(device(axis, delta, core))
     for peer in peers:
         pl.semaphore_signal(barrier, inc=1, device_id=peer, device_id_type=MESH)
+
+    chunk = 32
+    loads = []
+    for i in range(ROWS // chunk):
+        rows = pl.ds(i * chunk, chunk)
+        group = []
+        for n, (src, dst) in enumerate(((g_hbm, gv), (m_hbm, mv), (e_hbm, ev))):
+            copy = pltpu.make_async_copy(src.at[rows], dst.at[rows], in_sem.at[n, i])
+            copy.start()
+            group.append(copy)
+        loads.append(group)
+
+    even = lax.broadcasted_iota(jnp.int32, (8, LANES), 0) % 2 == 0
+    for i in range(ROWS // chunk):
+        for copy in loads[i]:
+            copy.wait()
+        rows = pl.ds(i * chunk, chunk)
+
+        def square(t, acc, rows=rows):
+            cols = lane_tile(t * LANES)
+            value = (
+                0.875 * mv[rows, cols].astype(F32)
+                + 0.125 * gv[rows, cols].astype(F32)
+                + ev[rows, cols].astype(F32)
+            )
+            comb[rows, cols] = value
+            return acc + value * value
+
+        acc = lax.fori_loop(0, COLS // LANES, square, jnp.zeros((chunk, LANES), F32), unroll=4)
+        for s in range(chunk // 8):
+            row = jnp.sum(acc[8 * s : 8 * s + 8], axis=1, keepdims=True)
+            row = jnp.broadcast_to(row, (8, LANES))
+            both = row + jnp.where(even, pltpu.roll(row, 7, 0), pltpu.roll(row, 1, 0))
+            rounded = jnp.sqrt(both * (1.0 / N_BLOCK)).astype(BF16)
+            scale[pl.ds(i * chunk + 8 * s, 8)] = rounded.astype(F32)
+
+    se_copy = pltpu.make_async_copy(se_hbm, se, aux_sem.at[0])
+    v_copy = pltpu.make_async_copy(v_hbm, vv, aux_sem.at[1])
+    p_copy = pltpu.make_async_copy(p_hbm, pv, aux_sem.at[2])
+    for copy in (se_copy, v_copy, p_copy):
+        copy.start()
     pl.semaphore_wait(barrier, len(peers))
 
     partner = device(0, 0, other)
     ring = [tuple(step(pos[order[0]], d) for d in range(4)) for order in ORDERS]
 
-    for k, order in enumerate(ORDERS):
-        p2 = ring[k][2]
-        for h in range(2):
+    for h in range(2):
+        for k, order in enumerate(ORDERS):
+            piece = 2 * k + h
+
+            def column(j, carry, piece=piece, k=k, h=h):
+                src, dst = lane_tile(piece * W + j * LANES), lane_tile(j * LANES)
+                for outer in range(4):
+                    tiles = []
+                    for inner in range(4):
+                        x, z = (inner, outer) if k == 1 else (outer, inner)
+                        parts = []
+                        for s in range(2):
+                            rows = pl.ds(16 * (4 * x + z) + 8 * s, 8)
+                            size = scale[rows]
+                            parts.append(jnp.where(comb[rows, src] >= 0, size, -size))
+                        tiles.append(parts)
+                    if k != 0:
+                        tiles = swap_granules(tiles)
+                    for i in range(4):
+                        far, near = (i, outer) if k == 2 else (outer, i)
+                        half, row = 2 * far + near // 2, (near % 2) * 16
+                        o[k, h, half, pl.ds(row, 16), dst] = jnp.concatenate(tiles[i], 0).astype(BF16)
+                return carry
+
+            lax.fori_loop(0, WIDTHS[piece] // LANES, column, 0)
+            if WIDTHS[piece] < W:
+                spare = W - WIDTHS[piece]
+                for half in range(8):
+                    o[k, h, half, :, pl.ds(WIDTHS[piece], spare)] = jnp.zeros((32, spare), BF16)
+            p2 = ring[k][2]
             push(o.at[k, h, 2 * p2], ra.at[k, 0, c], ra_sem.at[k, 0, c], device(order[0], 1, h))
             push(o.at[k, h, 2 * p2 + 1], ra.at[k, 1, c], ra_sem.at[k, 1, c], device(order[0], 3, h))
     for k, order in enumerate(ORDERS):
@@ -177,6 +170,16 @@
             push(o.at[k, h, 2 * p3], rb1.at[k, 1, c], rb1_sem.at[k, 1, c], device(order[0], 3, h))
     for k in range(3):
         push(o.at[k, other, pl.ds(2 * ring[k][0], 2)], ro.at[k], rd_sem.at[k, 2], partner)
+    def rest_column(j, carry):
+        cols = lane_tile(j * LANES)
+        for top in range(0, ROWS, 16):
+            rows = pl.ds(top, 16)
+            value, size = comb[rows, cols], scale[rows]
+            wn[rows, cols] = (value - jnp.where(value >= 0, size, -size)).astype(BF16)
+        return carry
+
+    lax.fori_loop(0, COLS // LANES, rest_column, 0)
+
     for k, order in enumerate(ORDERS):
         p, p1, _, p3 = ring[k]
         for d in range(2):
@@ -210,6 +213,16 @@
             push(
                 s1.at[k, step(q, delta)], r2.at[k, delta - 1], r2_sem.at[k, delta - 1], device(order[1], delta, c)
             )
+
+    def rate_column(j, carry):
+        cols = lane_tile(j * LANES)
+        for top in range(0, ROWS, 16):
+            rows = pl.ds(top, 16)
+            rate[rows, cols] = 0.5 / (jnp.sqrt(vv[rows, cols].astype(F32)) + 1e-08)
+        return carry
+
+    v_copy.wait()
+    lax.fori_loop(0, COLS // LANES, rate_column, 0)
 
     for k, order in enumerate(ORDERS):
         q, r = pos[order[1]], pos[order[2]]
@@ -227,6 +240,7 @@
         push(s2.at[k, 2 * r + other], r3.at[k, 0, c], r3_sem.at[k, 0, c], partner)
         r3[k, 0, c] = s2[k, 2 * r + c]
 
+    se_copy.wait()
     squares = jnp.zeros((2, LANES), F32)
     for piece in range(6):
         k, h = divmod(piece, 2)
@@ -311,74 +325,75 @@
             arrived(m.at[k, other, at], d_sem.at[k, n])
         for d in range(2):
             arrived(m.at[k, other, p2, pl.ds(2 * d, 2)], d_sem.at[k, 3 + d])
+    p_copy.wait()
     for copy in sent:
         copy.wait_send()
 
 
-def update_kernel(m, params, variance, params_next, momentum_next):
-    piece = pl.program_id(0)
-
-    for k in range(3):
-
-        @pl.when(piece // 2 == k)
-        def _(k=k):
-            def column(j, carry):
-                cols = lane_tile(j * LANES)
-                for outer in range(4):
-                    tiles = []
-                    for i in range(4):
-                        far, near = (i, outer) if k == 2 else (outer, i)
-                        tile = m[0, 0, far, near, :, cols].astype(F32)
-                        tiles.append([tile[:8], tile[8:]])
-                    if k != 0:
-                        tiles = swap_granules(tiles)
-                    for inner in range(4):
-                        x, z = (inner, outer) if k == 1 else (outer, inner)
-                        rows = pl.ds(16 * (4 * x + z), 16)
-                        value = jnp.concatenate(tiles[inner], 0)
-                        momentum_next[rows, cols] = value.astype(BF16)
-                        denom = jnp.sqrt(variance[rows, cols].astype(F32)) + 1e-08
-                        params_next[rows, cols] = params[rows, cols] - 0.5 * value / denom
-                return carry
-
-            lax.fori_loop(0, W // LANES, column, 0)
+def update_kernel(m, wn, sn, rate, pv, params_next, momentum_next, worker_next, server_next, pn, mn, sem):
+    stores = [
+        pltpu.make_async_copy(wn, worker_next, sem.at[0]),
+        pltpu.make_async_copy(sn, server_next, sem.at[1]),
+    ]
+    for copy in stores:
+        copy.start()
+    for piece in range(6):
+        k, h = divmod(piece, 2)
+
+        def column(j, carry, piece=piece, k=k, h=h):
+            src, dst = lane_tile(j * LANES), lane_tile(piece * W + j * LANES)
+            for outer in range(4):
+                tiles = []
+                for i in range(4):
+                    far, near = (i, outer) if k == 2 else (outer, i)
+                    tile = m[k, h, far, near, :, src].astype(F32)
+                    tiles.append([tile[:8], tile[8:]])
+                if k != 0:
+                    tiles = swap_granules(tiles)
+                for inner in range(4):
+                    x, z = (inner, outer) if k == 1 else (outer, inner)
+                    rows = pl.ds(16 * (4 * x + z), 16)
+                    value = jnp.concatenate(tiles[inner], 0)
+                    mn[rows, dst] = value.astype(BF16)
+                    pn[rows, dst] = pv[rows, dst] - value * rate[rows, dst]
+            return carry
+
+        lax.fori_loop(0, WIDTHS[piece] // LANES, column, 0)
+        cols = pl.ds(piece * W, WIDTHS[piece])
+        for n, (src, dst) in enumerate(((pn, params_next), (mn, momentum_next))):
+            copy = pltpu.make_async_copy(src.at[:, cols], dst.at[:, cols], sem.at[2 + 2 * piece + n])
+            copy.start()
+            stores.append(copy)
+    for copy in stores:
+        copy.wait()
 
 
 def local(gradients, momentum, worker_error, server_error, params, variance):
-    hbm = pl.BlockSpec(memory_space=pl.ANY)
+    hbm = pl.BlockSpec(memory_space=pltpu.HBM)
     vmem = pl.BlockSpec(memory_space=pltpu.VMEM)
-    worker_next, outgoing = pl.pallas_call(
-        compress_kernel,
+    dma = pltpu.SemaphoreType.DMA
+    whole = (ROWS, COLS)
+    own = (ROWS // N_DEV, COLS)
+    gathered, server_next, worker_next, rate, held = pl.pallas_call(
+        step_kernel,
         out_shape=(
-            jax.ShapeDtypeStruct((ROWS, COLS), BF16),
-            jax.ShapeDtypeStruct((3, 2, 8, 32, W), BF16),
+            pltpu.VMEM((3, 2, 4, 4, 16, W), BF16),
+            pltpu.VMEM(own, BF16),
+            pltpu.VMEM(whole, BF16),
+            pltpu.VMEM(whole, F32),
+            pltpu.VMEM(whole, F32),
         ),
-        in_specs=[hbm] * 3,
-        out_specs=(hbm, vmem),
+        in_specs=[hbm] * 6,
+        out_specs=(vmem,) * 5,
         scratch_shapes=[
-            pltpu.VMEM((ROWS, COLS), BF16),
-            pltpu.VMEM((ROWS, COLS), BF16),
-            pltpu.VMEM((ROWS, COLS), BF16),
-            pltpu.VMEM((ROWS, COLS), F32),
+            pltpu.VMEM(whole, BF16),
+            pltpu.VMEM(whole, BF16),
+            pltpu.VMEM(whole, BF16),
+            pltpu.VMEM(whole, BF16),
+            pltpu.VMEM(own, BF16),
+            pltpu.VMEM(whole, F32),
             pltpu.VMEM((ROWS, LANES), F32),
-            pltpu.VMEM((ROWS, COLS), BF16),
-            pltpu.SemaphoreType.DMA((3, 8)),
-            pltpu.SemaphoreType.DMA((6,)),
-        ],
-        compiler_params=pltpu.CompilerParams(vmem_limit_bytes=26 * 2**20),
-        name="compress",
-    )(gradients.reshape(ROWS, COLS), momentum, worker_error.reshape(ROWS, COLS))
-
-    dma = pltpu.SemaphoreType.DMA
-    gathered, server_next = pl.pallas_call(
-        exchange_kernel,
-        out_shape=(
-            jax.ShapeDtypeStruct((3, 2, 4, 4, 16, W), BF16),
-            jax.ShapeDtypeStruct((2, COLS), BF16),
-        ),
-        in_specs=[vmem, vmem],
-        out_specs=(vmem, vmem),
-        scratch_shapes=[
+            pltpu.VMEM((3, 2, 8, 32, W), BF16),
             pltpu.VMEM((3, 2, 2, 32, W), BF16),
             pltpu.VMEM((3, 2, 32, W), BF16),
             pltpu.VMEM((3, 2, 32, W), BF16),
@@ -393,6 +408,8 @@
             pltpu.VMEM((6, 2, W), F32),
             pltpu.VMEM((3, 2, 2, W), BF16),
             pltpu.VMEM((3, 8, 2, W), BF16),
+            dma((3, 8)),
+            dma((3,)),
             dma((N_SEND,)),
             dma((3, 2, 2)),
             dma((3, 3)),
@@ -406,30 +423,37 @@
             dma((3, 5)),
         ],
         compiler_params=pltpu.CompilerParams(
-            collective_id=0, has_side_effects=True, vmem_limit_bytes=20 * 2**20
+            collective_id=0, has_side_effects=True, vmem_limit_bytes=VMEM_STEP
         ),
-        name="exchange",
-    )(outgoing, server_error)
-
-    params_next, momentum_next = pl.pallas_call(
+        name="step",
+    )(
+        *(
+            pltpu.with_memory_space_constraint(a, pltpu.HBM)
+            for a in (
+                gradients.reshape(whole), momentum, worker_error.reshape(whole), server_error, params, variance
+            )
+        )
+    )
+
+    params_next, momentum_next, worker_next, server_next = pl.pallas_call(
         update_kernel,
-        grid=(6,),
         out_shape=(
-            jax.ShapeDtypeStruct((ROWS, COLS), F32),
-            jax.ShapeDtypeStruct((ROWS, COLS), BF16),
+            jax.ShapeDtypeStruct(whole, F32),
+            jax.ShapeDtypeStruct(whole, BF16),
+            jax.ShapeDtypeStruct(whole, BF16),
+            jax.ShapeDtypeStruct(own, BF16),
         ),
-        in_specs=[
-            pl.BlockSpec((1, 1, 4, 4, 16, W), lambda i: (i // 2, i % 2, 0, 0, 0, 0)),
-            pl.BlockSpec((ROWS, W), lambda i: (0, i)),
-            pl.BlockSpec((ROWS, W), lambda i: (0, i)),
-        ],
-        out_specs=(
-            pl.BlockSpec((ROWS, W), lambda i: (0, i)),
-            pl.BlockSpec((ROWS, W), lambda i: (0, i)),
-        ),
-        compiler_params=pltpu.CompilerParams(vmem_limit_bytes=16 * 2**20),
+        in_specs=[vmem] * 5,
+        out_specs=(hbm,) * 4,
+        scratch_shapes=[pltpu.VMEM(whole, F32), pltpu.VMEM(whole, BF16), dma((14,))],
+        compiler_params=pltpu.CompilerParams(vmem_limit_bytes=VMEM_UPDATE),
         name="update",
-    )(gathered, params, variance)
+    )(
+        *(
+            pltpu.with_memory_space_constraint(a, pltpu.VMEM)
+            for a in (gathered, worker_next, server_next, rate, held)
+        )
+    )
     return (params_next, momentum_next, worker_next.reshape(1, ROWS, COLS), server_next)
 
 

time: 67 us -> 54.1 us (0.81)
  Pallas kernels: 60 us -> 53.4 us
  local copies, waits for them, and re-layouts: 6.13 us -> 0 us
    pallas_call x3 -> x2, Pallas kernels: 60 us -> 53.4 us  [the longest x1 49.3 us: local(): pl.pallas_call(step_kernel, out_shape=(pltpu.VMEM((3, 2, 4, 4, 16, W), BF...]
    unnamed x15 -> x0, local copies, waits for them, and re-layouts: 6.13 us -> none
where the time goes in v2:
time: 54.1 us; the launch traced here: 54 us
  Pallas kernels  53.4 us (99%)
  between operations  0.64 us (1%)
    pallas_call x1, Pallas kernels, local(): pl.pallas_call(step_kernel, out_shape=(pltpu.VMEM((3, 2, 4, 4, 16, W), BF...  49.3 us
    pallas_call x1, Pallas kernels, local(): pl.pallas_call(update_kernel, out_shape=(jax.ShapeDtypeStruct(whole, F32)...  4.05 us

profile of v2, /device:TPU:1, one launch (start us, length us, event | category | flops | bytes accessed | tf_op | source)
XLA Modules:
  0.0 54.0 jit_solution(13467866464404071842)
XLA Ops:
  0.6 49.3 %step.1 = (bf16[3,2,4,4,16,896]{5,4,3,2,1,0:T(8,128)(2,1)S(1)}, bf16[2,5120]{1,0:T(2,128)(2,1)S(1)}, bf16[256,5120]{1,0:T(8,128)(2,1)S(1)}, f32[256,5120]{1,0:T(8,128)S(1)}, f32[256,5120]{1,0:T(8,128)S(1)}) custom-call(bf16[256,5120]{1,0:T(8,128)(2,1)} %bitcast.3, bf16[256,5120]{1,0:T(8,128)(2,1)} %m_hbm.1, bf16[256,5120]{1,0:T(8,128)(2,1)} %bitcast.4, ...), custom_call_target="tpu_custom_call" | custom-call | tf_op jit(solution)/shard_map/step/pallas_call | solution.py:377
  50.0 4.1 %update.1 = (f32[256,5120]{1,0:T(8,128)}, bf16[256,5120]{1,0:T(8,128)(2,1)}, bf16[256,5120]{1,0:T(8,128)(2,1)}, bf16[2,5120]{1,0:T(2,128)(2,1)}) custom-call(bf16[3,2,4,4,16,896]{5,4,3,2,1,0:T(8,128)(2,1)S(1)} %get-tuple-element.13.m, bf16[256,5120]{1,0:T(8,128)(2,1)S(1)} %get-tuple-element.14.wn, bf16[2,5120]{1,0:T(2,128)(2,1)S(1)} %get-tuple-element.15.sn, ...), custom_call_target="tpu_custom_call" | custom-call | tf_op jit(solution)/shard_map/update/pallas_call | solution.py:438

commit v3 on v2

v3 whole, which is shorter than its diff:
```python
import jax
import jax.numpy as jnp
from jax import lax
from jax.experimental import pallas as pl
from jax.experimental.pallas import tpu as pltpu
from jax.sharding import Mesh
from jax.sharding import PartitionSpec as P

MESH = pl.DeviceIdType.MESH
F32, BF16 = jnp.float32, jnp.bfloat16
DP = ("dp_0", "dp_1", "dp_2", "dp_3")
ORDERS = ((0, 1, 2), (1, 2, 0), (2, 0, 1))
ROWS, COLS, N_DEV = 256, 5120, 128
LANES = 128
W = 7 * LANES
WIDTHS = (W, W, W, W, W, COLS - 5 * W)
N_BLOCK = (ROWS // N_DEV) * COLS
CHUNK = 64
VMEM_STEP, VMEM_UPDATE = 26 * 2**20, 9 * 2**20


def lane_tile(start):
    return pl.ds(pl.multiple_of(start, LANES), LANES)


def swap_granules(tiles):
    low = lax.broadcasted_iota(jnp.int32, (8, LANES), 0) < 4
    swapped = []
    for i in range(4):
        pairs = []
        for first, second in ((tiles[0], tiles[1]), (tiles[2], tiles[3])):
            a, b = first[i // 2], second[i // 2]
            if i % 2 == 0:
                pairs.append(jnp.where(low, a, pltpu.roll(b, 4, 0)))
            else:
                pairs.append(jnp.where(low, pltpu.roll(a, 4, 0), b))
        swapped.append(pairs)
    return swapped


def step_kernel(
    g_hbm, m_hbm, e_hbm, se_hbm, p_hbm, v_hbm, m, sn, wn, rate, pv,
    gme, vv, se, comb, scale, o, ra, rb1, rb2, sb2, s1, r2, st, s2, r3, sv, mb, rq,
    in_sem, aux_sem, send_sem, ra_sem, rb1_sem, rb2_sem, r2_sem, r3_sem, rq_sem, q2_sem, q3_sem, d_sem,
):
    pos = [lax.axis_index(DP[a]) for a in range(3)]
    c = lax.axis_index(DP[3])
    other = 1 - c

    def step(v, d):
        return lax.rem(v + d, 4)

    def device(axis, delta, core):
        at = list(pos)
        if delta:
            at[axis] = step(pos[axis], delta)
        return (*at, core)

    def push(stage, src, dst, sem, to):
        pltpu.make_async_remote_copy(
            src_ref=src, dst_ref=dst, send_sem=send_sem.at[stage], recv_sem=sem,
            device_id=to, device_id_type=MESH,
        ).start()

    def left(stage, alike):
        pltpu.make_async_remote_copy(
            src_ref=alike, dst_ref=alike, send_sem=send_sem.at[stage], recv_sem=d_sem.at[0],
            device_id=device(0, 0, other), device_id_type=MESH,
        ).wait_send()

    def arrived(dst, sem):
        pltpu.make_async_remote_copy(
            src_ref=dst, dst_ref=dst, send_sem=send_sem.at[0], recv_sem=sem,
            device_id=device(0, 0, other), device_id_type=MESH,
        ).wait_recv()

    barrier = pltpu.get_barrier_semaphore()
    peers = [device(0, 0, other)]
    for axis in range(3):
        for delta in (1, 3, 2):
            for core in range(2):
                peers.append(device(axis, delta, core))
    for peer in peers:
        pl.semaphore_signal(barrier, inc=1, device_id=peer, device_id_type=MESH)

    for i in range(ROWS // CHUNK):
        rows = pl.ds(i * CHUNK, CHUNK)
        for n, src in enumerate((g_hbm, m_hbm, e_hbm)):
            pltpu.make_async_copy(src.at[rows], gme.at[n, rows], in_sem.at[i]).start()

    even = lax.broadcasted_iota(jnp.int32, (8, LANES), 0) % 2 == 0
    for i in range(ROWS // CHUNK):
        rows = pl.ds(i * CHUNK, CHUNK)
        pltpu.make_async_copy(gme.at[:, rows], gme.at[:, rows], in_sem.at[i]).wait()

        def square(t, acc, rows=rows):
            cols = lane_tile(t * LANES)
            value = (
                0.875 * gme[1, rows, cols].astype(F32)
                + 0.125 * gme[0, rows, cols].astype(F32)
                + gme[2, rows, cols].astype(F32)
            )
            comb[rows, cols] = value
            return acc + value * value

        acc = lax.fori_loop(0, COLS // LANES, square, jnp.zeros((CHUNK, LANES), F32), unroll=4)
        for s in range(CHUNK // 8):
            row = jnp.sum(acc[8 * s : 8 * s + 8], axis=1, keepdims=True)
            row = jnp.broadcast_to(row, (8, LANES))
            both = row + jnp.where(even, pltpu.roll(row, 7, 0), pltpu.roll(row, 1, 0))
            rounded = jnp.sqrt(both * (1.0 / N_BLOCK)).astype(BF16)
            scale[pl.ds(i * CHUNK + 8 * s, 8)] = rounded.astype(F32)

    se_copy = pltpu.make_async_copy(se_hbm, se, aux_sem.at[0])
    v_copy = pltpu.make_async_copy(v_hbm, vv, aux_sem.at[1])
    p_copy = pltpu.make_async_copy(p_hbm, pv, aux_sem.at[2])
    for copy in (se_copy, v_copy, p_copy):
        copy.start()
    pl.semaphore_wait(barrier, len(peers))

    partner = device(0, 0, other)
    ring = [tuple(step(pos[order[0]], d) for d in range(4)) for order in ORDERS]

    for h in range(2):
        for k, order in enumerate(ORDERS):
            piece = 2 * k + h

            def column(j, carry, piece=piece, k=k, h=h):
                src, dst = lane_tile(piece * W + j * LANES), lane_tile(j * LANES)
                for outer in range(4):
                    tiles = []
                    for inner in range(4):
                        x, z = (inner, outer) if k == 1 else (outer, inner)
                        parts = []
                        for s in range(2):
                            rows = pl.ds(16 * (4 * x + z) + 8 * s, 8)
                            size = scale[rows]
                            parts.append(jnp.where(comb[rows, src] >= 0, size, -size))
                        tiles.append(parts)
                    if k != 0:
                        tiles = swap_granules(tiles)
                    for i in range(4):
                        far, near = (i, outer) if k == 2 else (outer, i)
                        half, row = 2 * far + near // 2, (near % 2) * 16
                        o[k, h, half, pl.ds(row, 16), dst] = jnp.concatenate(tiles[i], 0).astype(BF16)
                return carry

            lax.fori_loop(0, WIDTHS[piece] // LANES, column, 0)
            if WIDTHS[piece] < W:
                spare = W - WIDTHS[piece]
                for half in range(8):
                    o[k, h, half, :, pl.ds(WIDTHS[piece], spare)] = jnp.zeros((32, spare), BF16)
            p2 = ring[k][2]
            push(0, o.at[k, h, 2 * p2], ra.at[k, 0, c], ra_sem.at[k, 0], device(order[0], 1, h))
            push(0, o.at[k, h, 2 * p2 + 1], ra.at[k, 1, c], ra_sem.at[k, 1], device(order[0], 3, h))
    for k, order in enumerate(ORDERS):
        p, p1, _, p3 = ring[k]
        push(0, o.at[k, other, 2 * p1], ra.at[k, 0, 2], ra_sem.at[k, 0], partner)
        push(0, o.at[k, other, 2 * p3 + 1], ra.at[k, 1, 2], ra_sem.at[k, 1], partner)
    for k, order in enumerate(ORDERS):
        p, p1, _, p3 = ring[k]
        for h in range(2):
            push(1, o.at[k, h, 2 * p1 + 1], rb1.at[k, c], rb1_sem.at[k], device(order[0], 1, h))
            push(1, o.at[k, h, 2 * p3], rb1.at[k, 2 + c], rb1_sem.at[k], device(order[0], 3, h))
    for k in range(3):
        push(1, o.at[k, other, pl.ds(2 * ring[k][0], 2)], rb1.at[k, pl.ds(4, 2)], rb1_sem.at[k], partner)

    def rest_column(j, carry):
        cols = lane_tile(j * LANES)
        for top in range(0, ROWS, 16):
            rows = pl.ds(top, 16)
            value, size = comb[rows, cols], scale[rows]
            wn[rows, cols] = (value - jnp.where(value >= 0, size, -size)).astype(BF16)
        return carry

    lax.fori_loop(0, COLS // LANES, rest_column, 0)

    for k, order in enumerate(ORDERS):
        p, p1, _, p3 = ring[k]
        for d in range(2):
            arrived(ra.at[k, d], ra_sem.at[k, d])
            for half in range(2):
                rows = pl.ds(16 * half, 16)
                sb2[k, d, rows] = (
                    (o[k, c, 2 * p1 if d == 0 else 2 * p3 + 1, rows].astype(F32) + ra[k, d, 2, rows].astype(F32))
                    + (ra[k, d, 0, rows].astype(F32) + ra[k, d, 1, rows].astype(F32))
                )
            push(2, sb2.at[k, d], rb2.at[k, d], rb2_sem.at[k], device(order[0], 1 if d == 0 else 3, c))

    for k, order in enumerate(ORDERS):
        p, q = ring[k][0], pos[order[1]]
        arrived(rb1.at[k], rb1_sem.at[k])
        arrived(rb2.at[k], rb2_sem.at[k])
        for d in range(2):
            for half in range(2):
                rows = pl.ds(16 * half, 16)
                s1[k, 2 * d + half] = (
                    (o[k, c, 2 * p + d, rows].astype(F32) + rb1[k, 4 + d, rows].astype(F32))
                    + (rb1[k, 2 - 2 * d, rows].astype(F32) + rb1[k, 3 - 2 * d, rows].astype(F32))
                    + rb2[k, d, rows]
                )
        for delta in (2, 1, 3):
            push(3, s1.at[k, step(q, delta)], r2.at[k, delta - 1], r2_sem.at[k], device(order[1], delta, c))

    def rate_column(j, carry):
        cols = lane_tile(j * LANES)
        for top in range(0, ROWS, 16):
            rows = pl.ds(top, 16)
            rate[rows, cols] = 0.5 / (jnp.sqrt(vv[rows, cols].astype(F32)) + 1e-08)
        return carry

    v_copy.wait()
    lax.fori_loop(0, COLS // LANES, rate_column, 0)

    for k, order in enumerate(ORDERS):
        q, r = pos[order[1]], pos[order[2]]
        arrived(r2.at[k], r2_sem.at[k])
        st[k] = (s1[k, q] + r2[k, 0]) + (r2[k, 1] + r2[k, 2])
        for i in range(8):
            s2[k, i] = st[k, pl.ds(2 * i, 2), :]
        for delta in (2, 1, 3):
            for core in range(2):
                src, dst = s2.at[k, 2 * step(r, delta) + core], r3.at[k, 2 * delta + c]
                push(4, src, dst, r3_sem.at[k], device(order[2], delta, core))
        push(4, s2.at[k, 2 * r + other], r3.at[k, c], r3_sem.at[k], partner)
        r3[k, c] = s2[k, 2 * r + c]

    se_copy.wait()
    squares = jnp.zeros((2, LANES), F32)
    for piece in range(6):
        k, h = divmod(piece, 2)
        if h == 0:
            arrived(r3.at[k, pl.ds(0, 7)], r3_sem.at[k])
        width = WIDTHS[piece]
        cols = pl.ds(0, width)
        total = (r3[k, h, :, cols] + r3[k, 2 + h, :, cols]) + (r3[k, 4 + h, :, cols] + r3[k, 6 + h, :, cols])
        served = total * (1.0 / N_DEV) + se[:, pl.ds(piece * W, width)].astype(F32)
        sv[piece, :, cols] = served
        for t in range(width // LANES):
            part = served[:, t * LANES : (t + 1) * LANES]
            squares = squares + part * part
    total = jnp.sum(jnp.sum(squares, axis=1, keepdims=True), axis=0, keepdims=True)
    size = jnp.sqrt(total * (1.0 / N_BLOCK)).astype(BF16).astype(F32)
    for piece in range(6):
        k, h = divmod(piece, 2)
        width = WIDTHS[piece]
        cols = pl.ds(0, width)
        served = sv[piece, :, cols]
        level = jnp.broadcast_to(size, (2, width))
        comp = jnp.where(served >= 0, level, -level)
        sn[:, pl.ds(piece * W, width)] = (served - comp).astype(BF16)
        mb[k, h, :, cols] = comp.astype(BF16)
        if width < W:
            mb[k, h, :, pl.ds(width, W - width)] = jnp.zeros((2, W - width), BF16)

    for k, order in enumerate(ORDERS):
        r = pos[order[2]]
        mine = 2 * r + c
        for delta in (2, 1, 3):
            for h in range(2):
                push(5, mb.at[k, h], rq.at[k, mine], rq_sem.at[k], device(order[2], delta, h))
        push(5, mb.at[k, other], rq.at[k, mine], rq_sem.at[k], partner)
        rq[k, mine] = mb[k, c]

    def spread(k, at, group):
        order = ORDERS[k]
        view = m.at[k, c, ring[k][0], at]
        for delta in (2, 1, 3):
            push(7, view, view, q3_sem.at[k, group, delta - 1], device(order[0], delta, c))
        push(8, view, view, d_sem.at[0], partner)

    for k, order in enumerate(ORDERS):
        p, q = pos[order[0]], pos[order[1]]
        arrived(rq.at[k, pl.ds(0, 7)], rq_sem.at[k])
        for i in range(8):
            st[k, pl.ds(2 * i, 2), :] = rq[k, i].astype(F32)
        m[k, c, p, q] = st[k].astype(BF16)
        view = m.at[k, c, p, q]
        for delta in (2, 1, 3):
            push(6, view, view, q2_sem.at[k, delta - 1], device(order[1], delta, c))
    for k, order in enumerate(ORDERS):
        spread(k, pos[order[1]], 0)
    for delta in (1, 3, 2):
        for k, order in enumerate(ORDERS):
            at = step(pos[order[1]], 4 - delta)
            arrived(m.at[k, c, pos[order[0]], at], q2_sem.at[k, delta - 1])
            spread(k, at, 1 if delta % 2 else 2)
    for group, tiles in enumerate(((0,), (1, 3), (2,))):
        for delta in (1, 3, 2):
            for k, order in enumerate(ORDERS):
                at, q = step(pos[order[0]], 4 - delta), pos[order[1]]
                arrived(m.at[k, c, at, pl.ds(0, len(tiles))], q3_sem.at[k, group, delta - 1])
                for shift in tiles:
                    view = m.at[k, c, at, step(q, shift)]
                    push(8, view, view, d_sem.at[0], partner)
    arrived(m.at[:, other], d_sem.at[0])
    p_copy.wait()
    for stage, alike in enumerate((
        ra, rb1, rb2, r2, r3.at[:, pl.ds(0, 7)], rq.at[:, pl.ds(0, 7)],
        m.at[:, 0, 0, pl.ds(0, 3)], m.at[:, 0, pl.ds(0, 3)], m.at[:, 0],
    )):
        left(stage, alike)


def update_kernel(m, wn, sn, rate, pv, params_next, momentum_next, worker_next, server_next, pn, mn, sem):
    whole = [
        pltpu.make_async_copy(wn, worker_next, sem.at[0]),
        pltpu.make_async_copy(sn, server_next, sem.at[1]),
    ]
    for copy in whole:
        copy.start()
    for piece in range(6):
        k, h = divmod(piece, 2)

        def column(j, carry, piece=piece, k=k, h=h):
            src, dst = lane_tile(j * LANES), lane_tile(piece * W + j * LANES)
            for outer in range(4):
                tiles = []
                for i in range(4):
                    far, near = (i, outer) if k == 2 else (outer, i)
                    tile = m[k, h, far, near, :, src].astype(F32)
                    tiles.append([tile[:8], tile[8:]])
                if k != 0:
                    tiles = swap_granules(tiles)
                for inner in range(4):
                    x, z = (inner, outer) if k == 1 else (outer, inner)
                    rows = pl.ds(16 * (4 * x + z), 16)
                    value = jnp.concatenate(tiles[inner], 0)
                    mn[rows, dst] = value.astype(BF16)
                    pn[rows, dst] = pv[rows, dst] - value * rate[rows, dst]
            return carry

        lax.fori_loop(0, WIDTHS[piece] // LANES, column, 0)
        cols = pl.ds(piece * W, WIDTHS[piece])
        pltpu.make_async_copy(pn.at[:, cols], params_next.at[:, cols], sem.at[2]).start()
        pltpu.make_async_copy(mn.at[:, cols], momentum_next.at[:, cols], sem.at[3]).start()
    whole += [
        pltpu.make_async_copy(pn, params_next, sem.at[2]),
        pltpu.make_async_copy(mn, momentum_next, sem.at[3]),
    ]
    for copy in whole:
        copy.wait()


def local(gradients, momentum, worker_error, server_error, params, variance):
    hbm = pl.BlockSpec(memory_space=pltpu.HBM)
    vmem = pl.BlockSpec(memory_space=pltpu.VMEM)
    dma = pltpu.SemaphoreType.DMA
    whole = (ROWS, COLS)
    own = (ROWS // N_DEV, COLS)
    gathered, server_next, worker_next, rate, held = pl.pallas_call(
        step_kernel,
        out_shape=(
            pltpu.VMEM((3, 2, 4, 4, 16, W), BF16),
            pltpu.VMEM(own, BF16),
            pltpu.VMEM(whole, BF16),
            pltpu.VMEM(whole, F32),
            pltpu.VMEM(whole, F32),
        ),
        in_specs=[hbm] * 6,
        out_specs=(vmem,) * 5,
        scratch_shapes=[
            pltpu.VMEM((3, ROWS, COLS), BF16),
            pltpu.VMEM(whole, BF16),
            pltpu.VMEM(own, BF16),
            pltpu.VMEM(whole, F32),
            pltpu.VMEM((ROWS, LANES), F32),
            pltpu.VMEM((3, 2, 8, 32, W), BF16),
            pltpu.VMEM((3, 2, 3, 32, W), BF16),
            pltpu.VMEM((3, 6, 32, W), BF16),
            pltpu.VMEM((3, 2, 32, W), F32),
            pltpu.VMEM((3, 2, 32, W), F32),
            pltpu.VMEM((3, 4, 16, W), F32),
            pltpu.VMEM((3, 3, 16, W), F32),
            pltpu.VMEM((3, 16, W), F32),
            pltpu.VMEM((3, 8, 2, W), F32),
            pltpu.VMEM((3, 8, 2, W), F32),
            pltpu.VMEM((6, 2, W), F32),
            pltpu.VMEM((3, 2, 2, W), BF16),
            pltpu.VMEM((3, 8, 2, W), BF16),
            dma((ROWS // CHUNK,)),
            dma((3,)),
            dma((9,)),
            dma((3, 2)),
            dma((3,)),
            dma((3,)),
            dma((3,)),
            dma((3,)),
            dma((3,)),
            dma((3, 3)),
            dma((3, 3, 3)),
            dma((1,)),
        ],
        compiler_params=pltpu.CompilerParams(
            collective_id=0, has_side_effects=True, vmem_limit_bytes=VMEM_STEP
        ),
        name="step",
    )(
        *(
            pltpu.with_memory_space_constraint(a, pltpu.HBM)
            for a in (
                gradients.reshape(whole), momentum, worker_error.reshape(whole), server_error, params, variance
            )
        )
    )

    params_next, momentum_next, worker_next, server_next = pl.pallas_call(
        update_kernel,
        out_shape=(
            jax.ShapeDtypeStruct(whole, F32),
            jax.ShapeDtypeStruct(whole, BF16),
            jax.ShapeDtypeStruct(whole, BF16),
            jax.ShapeDtypeStruct(own, BF16),
        ),
        in_specs=[vmem] * 5,
        out_specs=(hbm,) * 4,
        scratch_shapes=[pltpu.VMEM(whole, F32), pltpu.VMEM(whole, BF16), dma((4,))],
        compiler_params=pltpu.CompilerParams(vmem_limit_bytes=VMEM_UPDATE),
        name="update",
    )(
        *(
            pltpu.with_memory_space_constraint(a, pltpu.VMEM)
            for a in (gathered, worker_next, server_next, rate, held)
        )
    )
    return (params_next, momentum_next, worker_next.reshape(1, ROWS, COLS), server_next)


def solution(mesh):
    split = Mesh(mesh.devices.reshape(4, 4, 4, 2), DP)
    in_specs = (P(DP, None, None), P(), P(DP, None, None), P(DP, None), P(), P())
    out_specs = (P(), P(), P(DP, None, None), P(DP, None))
    return jax.shard_map(local, mesh=split, in_specs=in_specs, out_specs=out_specs, check_vma=False)
```

time: 54.1 us -> 49.5 us (0.915)
  Pallas kernels: 53.4 us -> 48.8 us
    pallas_call x1, Pallas kernels: 49.3 us -> 44.8 us  [local(): pl.pallas_call(step_kernel, out_shape=(pltpu.VMEM((3, 2, 4, 4, 16, W), BF...]
where the time goes in v3:
time: 49.5 us; the launch traced here: 49.4 us
  Pallas kernels  48.8 us (99%)
  between operations  0.64 us (1%)
    pallas_call x1, Pallas kernels, local(): pl.pallas_call(step_kernel, out_shape=(pltpu.VMEM((3, 2, 4, 4, 16, W), BF...  44.8 us
    pallas_call x1, Pallas kernels, local(): pl.pallas_call(update_kernel, out_shape=(jax.ShapeDtypeStruct(whole, F32)...  3.96 us

profile of v3, /device:TPU:1, one launch (start us, length us, event | category | flops | bytes accessed | tf_op | source)
XLA Modules:
  0.0 49.4 jit_solution(5853380395946057917)
XLA Ops:
  0.6 44.8 %step.1 = (bf16[3,2,4,4,16,896]{5,4,3,2,1,0:T(8,128)(2,1)S(1)}, bf16[2,5120]{1,0:T(2,128)(2,1)S(1)}, bf16[256,5120]{1,0:T(8,128)(2,1)S(1)}, f32[256,5120]{1,0:T(8,128)S(1)}, f32[256,5120]{1,0:T(8,128)S(1)}) custom-call(bf16[256,5120]{1,0:T(8,128)(2,1)} %bitcast.3, bf16[256,5120]{1,0:T(8,128)(2,1)} %m_hbm.1, bf16[256,5120]{1,0:T(8,128)(2,1)} %bitcast.4, ...), custom_call_target="tpu_custom_call" | custom-call | tf_op jit(solution)/shard_map/step/pallas_call | solution.py:351
  45.5 4.0 %update.1 = (f32[256,5120]{1,0:T(8,128)}, bf16[256,5120]{1,0:T(8,128)(2,1)}, bf16[256,5120]{1,0:T(8,128)(2,1)}, bf16[2,5120]{1,0:T(2,128)(2,1)}) custom-call(bf16[3,2,4,4,16,896]{5,4,3,2,1,0:T(8,128)(2,1)S(1)} %get-tuple-element.13.m, bf16[256,5120]{1,0:T(8,128)(2,1)S(1)} %get-tuple-element.14.wn, bf16[2,5120]{1,0:T(2,128)(2,1)S(1)} %get-tuple-element.15.sn, ...), custom_call_target="tpu_custom_call" | custom-call | tf_op jit(solution)/shard_map/update/pallas_call | solution.py:407

commit v4 on v3

--- a/solution.py
+++ b/solution.py
@@ -41,7 +41,7 @@
 def step_kernel(
     g_hbm, m_hbm, e_hbm, se_hbm, p_hbm, v_hbm, m, sn, wn, rate, pv,
     gme, vv, se, comb, scale, o, ra, rb1, rb2, sb2, s1, r2, st, s2, r3, sv, mb, rq,
-    in_sem, aux_sem, send_sem, ra_sem, rb1_sem, rb2_sem, r2_sem, r3_sem, rq_sem, q2_sem, q3_sem, d_sem,
+    in_sem, aux_sem, send_sem, ra_sem, rb1_sem, rb2_sem, r2_sem, r3_sem, rq_sem, q3_sem, d_sem,
 ):
     pos = [lax.axis_index(DP[a]) for a in range(3)]
     c = lax.axis_index(DP[3])
@@ -52,7 +52,7 @@
 
     def device(axis, delta, core):
         at = list(pos)
-        if delta:
+        if not isinstance(delta, int) or delta:
             at[axis] = step(pos[axis], delta)
         return (*at, core)
 
@@ -75,18 +75,20 @@
         ).wait_recv()
 
     barrier = pltpu.get_barrier_semaphore()
-    peers = [device(0, 0, other)]
-    for axis in range(3):
-        for delta in (1, 3, 2):
-            for core in range(2):
-                peers.append(device(axis, delta, core))
-    for peer in peers:
-        pl.semaphore_signal(barrier, inc=1, device_id=peer, device_id_type=MESH)
-
     for i in range(ROWS // CHUNK):
         rows = pl.ds(i * CHUNK, CHUNK)
         for n, src in enumerate((g_hbm, m_hbm, e_hbm)):
             pltpu.make_async_copy(src.at[rows], gme.at[n, rows], in_sem.at[i]).start()
+
+    peers = [(*pos, other)]
+    for x in range(4):
+        for z in range(4):
+            for y in range(4):
+                if x * z * y == 0 and x + z + y > 0:
+                    chip = (step(pos[0], x), step(pos[1], z), step(pos[2], y))
+                    peers += [(*chip, 0), (*chip, 1)]
+    for peer in peers:
+        pl.semaphore_signal(barrier, inc=1, device_id=peer, device_id_type=MESH)
 
     even = lax.broadcasted_iota(jnp.int32, (8, LANES), 0) % 2 == 0
     for i in range(ROWS // CHUNK):
@@ -103,7 +105,7 @@
             comb[rows, cols] = value
             return acc + value * value
 
-        acc = lax.fori_loop(0, COLS // LANES, square, jnp.zeros((CHUNK, LANES), F32), unroll=4)
+        acc = lax.fori_loop(0, COLS // LANES, square, jnp.zeros((CHUNK, LANES), F32), unroll=8)
         for s in range(CHUNK // 8):
             row = jnp.sum(acc[8 * s : 8 * s + 8], axis=1, keepdims=True)
             row = jnp.broadcast_to(row, (8, LANES))
@@ -175,32 +177,39 @@
 
     lax.fori_loop(0, COLS // LANES, rest_column, 0)
 
-    for k, order in enumerate(ORDERS):
-        p, p1, _, p3 = ring[k]
-        for d in range(2):
-            arrived(ra.at[k, d], ra_sem.at[k, d])
-            for half in range(2):
-                rows = pl.ds(16 * half, 16)
+    for half in range(2):
+        rows = pl.ds(16 * half, 16)
+        for k, order in enumerate(ORDERS):
+            p, p1, _, p3 = ring[k]
+            for d in range(2):
+                if half == 0:
+                    arrived(ra.at[k, d], ra_sem.at[k, d])
                 sb2[k, d, rows] = (
                     (o[k, c, 2 * p1 if d == 0 else 2 * p3 + 1, rows].astype(F32) + ra[k, d, 2, rows].astype(F32))
                     + (ra[k, d, 0, rows].astype(F32) + ra[k, d, 1, rows].astype(F32))
                 )
-            push(2, sb2.at[k, d], rb2.at[k, d], rb2_sem.at[k], device(order[0], 1 if d == 0 else 3, c))
-
-    for k, order in enumerate(ORDERS):
-        p, q = ring[k][0], pos[order[1]]
-        arrived(rb1.at[k], rb1_sem.at[k])
-        arrived(rb2.at[k], rb2_sem.at[k])
-        for d in range(2):
-            for half in range(2):
-                rows = pl.ds(16 * half, 16)
+                to = device(order[0], 1 if d == 0 else 3, c)
+                push(2, sb2.at[k, d, rows], rb2.at[k, d, rows], rb2_sem.at[k, half], to)
+
+    for half in range(2):
+        rows = pl.ds(16 * half, 16)
+        for k, order in enumerate(ORDERS):
+            p, q = ring[k][0], pos[order[1]]
+            if half == 0:
+                arrived(rb1.at[k], rb1_sem.at[k])
+            arrived(rb2.at[k, 0], rb2_sem.at[k, half])
+            for d in range(2):
                 s1[k, 2 * d + half] = (
                     (o[k, c, 2 * p + d, rows].astype(F32) + rb1[k, 4 + d, rows].astype(F32))
                     + (rb1[k, 2 - 2 * d, rows].astype(F32) + rb1[k, 3 - 2 * d, rows].astype(F32))
                     + rb2[k, d, rows]
                 )
-        for delta in (2, 1, 3):
-            push(3, s1.at[k, step(q, delta)], r2.at[k, delta - 1], r2_sem.at[k], device(order[1], delta, c))
+            for to in (half, 2 + half):
+
+                @pl.when(q != to)
+                def _(k=k, order=order, q=q, to=to):
+                    delta = step(to + 4, -q)
+                    push(3, s1.at[k, to], r2.at[k, delta - 1], r2_sem.at[k], device(order[1], delta, c))
 
     def rate_column(j, carry):
         cols = lane_tile(j * LANES)
@@ -253,51 +262,55 @@
         if width < W:
             mb[k, h, :, pl.ds(width, W - width)] = jnp.zeros((2, W - width), BF16)
 
-    for k, order in enumerate(ORDERS):
-        r = pos[order[2]]
-        mine = 2 * r + c
-        for delta in (2, 1, 3):
-            for h in range(2):
-                push(5, mb.at[k, h], rq.at[k, mine], rq_sem.at[k], device(order[2], delta, h))
-        push(5, mb.at[k, other], rq.at[k, mine], rq_sem.at[k], partner)
-        rq[k, mine] = mb[k, c]
+    def place(k, q_shift, r_shift, core):
+        at = list(pos)
+        at[ORDERS[k][1]] = step(at[ORDERS[k][1]], q_shift)
+        at[ORDERS[k][2]] = step(at[ORDERS[k][2]], r_shift)
+        return (*at, core)
+
+    for q_shift in (0, 1, 3, 2):
+        for r_shift in (2, 1, 3, 0):
+            for k, order in enumerate(ORDERS):
+                q, mine = pos[order[1]], 2 * pos[order[2]] + c
+                sem = rq_sem.at[k, (0, 1, 2, 1)[q_shift]]
+                if q_shift or r_shift:
+                    for h in range(2):
+                        push(8 if q_shift else 5, mb.at[k, h], rq.at[k, q, mine], sem, place(k, q_shift, r_shift, h))
+                else:
+                    push(5, mb.at[k, other], rq.at[k, q, mine], sem, partner)
+                    rq[k, q, mine] = mb[k, c]
 
     def spread(k, at, group):
         order = ORDERS[k]
         view = m.at[k, c, ring[k][0], at]
         for delta in (2, 1, 3):
-            push(7, view, view, q3_sem.at[k, group, delta - 1], device(order[0], delta, c))
-        push(8, view, view, d_sem.at[0], partner)
-
-    for k, order in enumerate(ORDERS):
-        p, q = pos[order[0]], pos[order[1]]
-        arrived(rq.at[k, pl.ds(0, 7)], rq_sem.at[k])
-        for i in range(8):
-            st[k, pl.ds(2 * i, 2), :] = rq[k, i].astype(F32)
-        m[k, c, p, q] = st[k].astype(BF16)
-        view = m.at[k, c, p, q]
-        for delta in (2, 1, 3):
-            push(6, view, view, q2_sem.at[k, delta - 1], device(order[1], delta, c))
-    for k, order in enumerate(ORDERS):
-        spread(k, pos[order[1]], 0)
-    for delta in (1, 3, 2):
+            push(6, view, view, q3_sem.at[k, group], device(order[0], delta, c))
+        push(7, view, view, d_sem.at[0], partner)
+
+    for group, shifts in enumerate(((0,), (1, 3), (2,))):
         for k, order in enumerate(ORDERS):
-            at = step(pos[order[1]], 4 - delta)
-            arrived(m.at[k, c, pos[order[0]], at], q2_sem.at[k, delta - 1])
-            spread(k, at, 1 if delta % 2 else 2)
+            q = pos[order[1]]
+            arrived(rq.at[k, 0, pl.ds(0, 7)] if group == 0 else rq.at[k, pl.ds(0, len(shifts))], rq_sem.at[k, group])
+            for shift in shifts:
+                at = step(q, shift)
+                for i in range(8):
+                    st[k, pl.ds(2 * i, 2), :] = rq[k, at, i].astype(F32)
+                m[k, c, pos[order[0]], at] = st[k].astype(BF16)
+            for shift in shifts:
+                spread(k, step(q, shift), group)
     for group, tiles in enumerate(((0,), (1, 3), (2,))):
-        for delta in (1, 3, 2):
-            for k, order in enumerate(ORDERS):
+        for k, order in enumerate(ORDERS):
+            arrived(m.at[k, 0, pl.ds(0, 3), pl.ds(0, len(tiles))], q3_sem.at[k, group])
+            for delta in (1, 3, 2):
                 at, q = step(pos[order[0]], 4 - delta), pos[order[1]]
-                arrived(m.at[k, c, at, pl.ds(0, len(tiles))], q3_sem.at[k, group, delta - 1])
                 for shift in tiles:
                     view = m.at[k, c, at, step(q, shift)]
-                    push(8, view, view, d_sem.at[0], partner)
+                    push(7, view, view, d_sem.at[0], partner)
     arrived(m.at[:, other], d_sem.at[0])
     p_copy.wait()
     for stage, alike in enumerate((
-        ra, rb1, rb2, r2, r3.at[:, pl.ds(0, 7)], rq.at[:, pl.ds(0, 7)],
-        m.at[:, 0, 0, pl.ds(0, 3)], m.at[:, 0, pl.ds(0, 3)], m.at[:, 0],
+        ra, rb1, rb2, r2, r3.at[:, pl.ds(0, 7)], rq.at[:, 0, pl.ds(0, 7)],
+        m.at[:, 0, pl.ds(0, 3)], m.at[:, 0], rq.at[:, pl.ds(0, 3)],
     )):
         left(stage, alike)
 
@@ -377,18 +390,17 @@
             pltpu.VMEM((3, 8, 2, W), F32),
             pltpu.VMEM((6, 2, W), F32),
             pltpu.VMEM((3, 2, 2, W), BF16),
-            pltpu.VMEM((3, 8, 2, W), BF16),
+            pltpu.VMEM((3, 4, 8, 2, W), BF16),
             dma((ROWS // CHUNK,)),
             dma((3,)),
             dma((9,)),
             dma((3, 2)),
             dma((3,)),
-            dma((3,)),
-            dma((3,)),
+            dma((3, 2)),
             dma((3,)),
             dma((3,)),
             dma((3, 3)),
-            dma((3, 3, 3)),
+            dma((3, 3)),
             dma((1,)),
         ],
         compiler_params=pltpu.CompilerParams(

time: 49.5 us -> 47.3 us (0.956)
  Pallas kernels: 48.8 us -> 46.6 us
    pallas_call x1, Pallas kernels: 44.8 us -> 42.6 us  [local(): pl.pallas_call(step_kernel, out_shape=(pltpu.VMEM((3, 2, 4, 4, 16, W), BF...]
where the time goes in v4:
time: 47.3 us; the launch traced here: 47.2 us
  Pallas kernels  46.6 us (99%)
  between operations  0.64 us (1%)
    pallas_call x1, Pallas kernels, local(): pl.pallas_call(step_kernel, out_shape=(pltpu.VMEM((3, 2, 4, 4, 16, W), BF...  42.6 us
    pallas_call x1, Pallas kernels, local(): pl.pallas_call(update_kernel, out_shape=(jax.ShapeDtypeStruct(whole, F32)...  3.96 us

profile of v4, /device:TPU:1, one launch (start us, length us, event | category | flops | bytes accessed | tf_op | source)
XLA Modules:
  0.0 47.2 jit_solution(13170190482995659288)
XLA Ops:
  0.6 42.6 %step.1 = (bf16[3,2,4,4,16,896]{5,4,3,2,1,0:T(8,128)(2,1)S(1)}, bf16[2,5120]{1,0:T(2,128)(2,1)S(1)}, bf16[256,5120]{1,0:T(8,128)(2,1)S(1)}, f32[256,5120]{1,0:T(8,128)S(1)}, f32[256,5120]{1,0:T(8,128)S(1)}) custom-call(bf16[256,5120]{1,0:T(8,128)(2,1)} %bitcast.3, bf16[256,5120]{1,0:T(8,128)(2,1)} %m_hbm.1, bf16[256,5120]{1,0:T(8,128)(2,1)} %bitcast.4, ...), custom_call_target="tpu_custom_call" | custom-call | tf_op jit(solution)/shard_map/step/pallas_call | solution.py:364
  43.2 4.0 %update.1 = (f32[256,5120]{1,0:T(8,128)}, bf16[256,5120]{1,0:T(8,128)(2,1)}, bf16[256,5120]{1,0:T(8,128)(2,1)}, bf16[2,5120]{1,0:T(2,128)(2,1)}) custom-call(bf16[3,2,4,4,16,896]{5,4,3,2,1,0:T(8,128)(2,1)S(1)} %get-tuple-element.13.m, bf16[256,5120]{1,0:T(8,128)(2,1)S(1)} %get-tuple-element.14.wn, bf16[2,5120]{1,0:T(2,128)(2,1)S(1)} %get-tuple-element.15.sn, ...), custom_call_target="tpu_custom_call" | custom-call | tf_op jit(solution)/shard_map/update/pallas_call | solution.py:419

commit v5 on v4

--- a/solution.py
+++ b/solution.py
@@ -284,7 +284,8 @@
         order = ORDERS[k]
         view = m.at[k, c, ring[k][0], at]
         for delta in (2, 1, 3):
-            push(6, view, view, q3_sem.at[k, group], device(order[0], delta, c))
+            sem = q3_sem.at[k, 3 if group == 2 and delta == 2 else group]
+            push(6, view, view, sem, device(order[0], delta, c))
         push(7, view, view, d_sem.at[0], partner)
 
     for group, shifts in enumerate(((0,), (1, 3), (2,))):
@@ -298,10 +299,10 @@
                 m[k, c, pos[order[0]], at] = st[k].astype(BF16)
             for shift in shifts:
                 spread(k, step(q, shift), group)
-    for group, tiles in enumerate(((0,), (1, 3), (2,))):
+    for group, (tiles, deltas) in enumerate((((0,), (1, 3, 2)), ((1, 3), (1, 3, 2)), ((2,), (1, 3)), ((2,), (2,)))):
         for k, order in enumerate(ORDERS):
-            arrived(m.at[k, 0, pl.ds(0, 3), pl.ds(0, len(tiles))], q3_sem.at[k, group])
-            for delta in (1, 3, 2):
+            arrived(m.at[k, 0, pl.ds(0, len(deltas)), pl.ds(0, len(tiles))], q3_sem.at[k, group])
+            for delta in deltas:
                 at, q = step(pos[order[0]], 4 - delta), pos[order[1]]
                 for shift in tiles:
                     view = m.at[k, c, at, step(q, shift)]
@@ -400,7 +401,7 @@
             dma((3,)),
             dma((3,)),
             dma((3, 3)),
-            dma((3, 3)),
+            dma((3, 4)),
             dma((1,)),
         ],
         compiler_params=pltpu.CompilerParams(

time: 47.3 us -> 47.3 us (level)
  no operation moved by 1% of the time
where the time goes in v5:
time: 47.3 us; the launch traced here: 47.2 us
  Pallas kernels  46.6 us (99%)
  between operations  0.64 us (1%)
    pallas_call x1, Pallas kernels, local(): pl.pallas_call(step_kernel, out_shape=(pltpu.VMEM((3, 2, 4, 4, 16, W), BF...  42.6 us
    pallas_call x1, Pallas kernels, local(): pl.pallas_call(update_kernel, out_shape=(jax.ShapeDtypeStruct(whole, F32)...  3.96 us

profile of v5, /device:TPU:1, one launch (start us, length us, event | category | flops | bytes accessed | tf_op | source)
XLA Modules:
  0.0 47.2 jit_solution(5286521560646912515)
XLA Ops:
  0.6 42.6 %step.1 = (bf16[3,2,4,4,16,896]{5,4,3,2,1,0:T(8,128)(2,1)S(1)}, bf16[2,5120]{1,0:T(2,128)(2,1)S(1)}, bf16[256,5120]{1,0:T(8,128)(2,1)S(1)}, f32[256,5120]{1,0:T(8,128)S(1)}, f32[256,5120]{1,0:T(8,128)S(1)}) custom-call(bf16[256,5120]{1,0:T(8,128)(2,1)} %bitcast.3, bf16[256,5120]{1,0:T(8,128)(2,1)} %m_hbm.1, bf16[256,5120]{1,0:T(8,128)(2,1)} %bitcast.4, ...), custom_call_target="tpu_custom_call" | custom-call | tf_op jit(solution)/shard_map/step/pallas_call | solution.py:365
  43.3 4.0 %update.1 = (f32[256,5120]{1,0:T(8,128)}, bf16[256,5120]{1,0:T(8,128)(2,1)}, bf16[256,5120]{1,0:T(8,128)(2,1)}, bf16[2,5120]{1,0:T(2,128)(2,1)}) custom-call(bf16[3,2,4,4,16,896]{5,4,3,2,1,0:T(8,128)(2,1)S(1)} %get-tuple-element.13.m, bf16[256,5120]{1,0:T(8,128)(2,1)S(1)} %get-tuple-element.14.wn, bf16[2,5120]{1,0:T(2,128)(2,1)S(1)} %get-tuple-element.15.sn, ...), custom_call_target="tpu_custom_call" | custom-call | tf_op jit(solution)/shard_map/update/pallas_call | solution.py:420

commit v6 on v4

--- a/solution.py
+++ b/solution.py
@@ -219,7 +219,6 @@
         return carry
 
     v_copy.wait()
-    lax.fori_loop(0, COLS // LANES, rate_column, 0)
 
     for k, order in enumerate(ORDERS):
         q, r = pos[order[1]], pos[order[2]]
@@ -287,6 +286,7 @@
             push(6, view, view, q3_sem.at[k, group], device(order[0], delta, c))
         push(7, view, view, d_sem.at[0], partner)
 
+    lax.fori_loop(0, COLS // LANES, rate_column, 0)
     for group, shifts in enumerate(((0,), (1, 3), (2,))):
         for k, order in enumerate(ORDERS):
             q = pos[order[1]]

time: 47.3 us -> 47.3 us (level)
  no operation moved by 1% of the time
where the time goes in v6:
time: 47.3 us; the launch traced here: 47.2 us
  Pallas kernels  46.6 us (99%)
  between operations  0.64 us (1%)
    pallas_call x1, Pallas kernels, local(): pl.pallas_call(step_kernel, out_shape=(pltpu.VMEM((3, 2, 4, 4, 16, W), BF...  42.6 us
    pallas_call x1, Pallas kernels, local(): pl.pallas_call(update_kernel, out_shape=(jax.ShapeDtypeStruct(whole, F32)...  3.96 us

profile of v6, /device:TPU:1, one launch (start us, length us, event | category | flops | bytes accessed | tf_op | source)
XLA Modules:
  0.0 47.2 jit_solution(13147038065048049690)
XLA Ops:
  0.6 42.6 %step.1 = (bf16[3,2,4,4,16,896]{5,4,3,2,1,0:T(8,128)(2,1)S(1)}, bf16[2,5120]{1,0:T(2,128)(2,1)S(1)}, bf16[256,5120]{1,0:T(8,128)(2,1)S(1)}, f32[256,5120]{1,0:T(8,128)S(1)}, f32[256,5120]{1,0:T(8,128)S(1)}) custom-call(bf16[256,5120]{1,0:T(8,128)(2,1)} %bitcast.3, bf16[256,5120]{1,0:T(8,128)(2,1)} %m_hbm.1, bf16[256,5120]{1,0:T(8,128)(2,1)} %bitcast.4, ...), custom_call_target="tpu_custom_call" | custom-call | tf_op jit(solution)/shard_map/step/pallas_call | solution.py:364
  43.2 4.0 %update.1 = (f32[256,5120]{1,0:T(8,128)}, bf16[256,5120]{1,0:T(8,128)(2,1)}, bf16[256,5120]{1,0:T(8,128)(2,1)}, bf16[2,5120]{1,0:T(2,128)(2,1)}) custom-call(bf16[3,2,4,4,16,896]{5,4,3,2,1,0:T(8,128)(2,1)S(1)} %get-tuple-element.13.m, bf16[256,5120]{1,0:T(8,128)(2,1)S(1)} %get-tuple-element.14.wn, bf16[2,5120]{1,0:T(2,128)(2,1)S(1)} %get-tuple-element.15.sn, ...), custom_call_target="tpu_custom_call" | custom-call | tf_op jit(solution)/shard_map/update/pallas_call | solution.py:419
